TPU v7x, 32 devices: a whole 2x2x4 slice. The times are simulated.
32 devices in a mesh: groups: 2 (over y), rows: 4 (over z), cols: 2 (over x), sub: 2 (over core).
Axes of the slice: x: 2, y: 2, z: 4, core: 2. Of those that a mesh axis runs over, the one named last changes fastest.
Arguments:
- returns: float32 [8, 64, 8192], P('groups', 'rows', ('cols', 'sub')), parts along dimension 0, may hold values from -6 to 6
- starts: int32 [8, 8192], P('groups', ('cols', 'sub')), parts along dimension 0, may hold values from 0 to 32
- start_block: float32 [8, 32, 8192], P('groups', None, ('cols', 'sub')), parts along dimension 0, may hold values from -6 to 6
Outputs:
- loadings: float32 [8, 32, 8192], P('groups', None, ('cols', 'sub')), parts along dimension 0
There are 2 independent parts, one for each index of `groups`. A program takes and returns all parts, laid end to end along the dimension named above; each array names one. Nothing has to cross between parts.
Inputs may be any that keep to these rules, and one draw needn't show every extreme that they name: `starts`: days before an asset's start day hold returns that do not count.
All inputs are finite; a program needn't handle non-finite values.
Results may differ from a plain program's by a relative error of at most 0.0078.
Values may be sent and summed in bfloat16 or wider, within the bound.
A program may use at most 64 MiB of HBM per device.

v0:
```python
import functools

import jax
import jax.numpy as jnp
from jax import lax
from jax.experimental import pallas as pl
from jax.experimental.pallas import tpu as pltpu
from jax.sharding import PartitionSpec as P

ITERS = 3
HIGHEST = lax.Precision.HIGHEST
MESH = pl.DeviceIdType.MESH
NT = (((1,), (1,)), ((), ()))
SUBLANES = 8


def eliminate(gram, right):
    size = gram.shape[0]
    height = min(SUBLANES, size)
    blocks = size // height
    gs = [gram[b * height:(b + 1) * height] for b in range(blocks)]
    rs = [right[b * height:(b + 1) * height] for b in range(blocks)]
    row_id = lax.broadcasted_iota(jnp.int32, (height, 1), 0)
    diag = [jnp.ones((height, right.shape[1]), jnp.float32) for _ in range(blocks)]
    wide = max(size, right.shape[1])
    for b in range(blocks):
        panel = {
            (c, i): jnp.broadcast_to(gs[c][:, b * height + i:b * height + i + 1], (height, wide))
            for c in range(b, blocks) for i in range(height)
        }
        for i in range(height):
            grow = gs[b][i:i + 1]
            rrow = rs[b][i:i + 1]
            pivot = panel[b, i][i:i + 1]
            diag[b] = jnp.where(row_id == i, pivot[:, :right.shape[1]], diag[b])
            inverse = 1.0 / pivot
            ahead = {n: panel[b, n][i:i + 1] for n in range(i + 1, height)}
            for c in range(b, blocks):
                factor = panel[c, i] * inverse
                if c == b:
                    factor = jnp.where(row_id > i, factor, 0.0)
                for n in range(i + 1, height):
                    panel[c, n] = panel[c, n] - factor * ahead[n]
                gs[c] = gs[c] - factor[:, :size] * grow
                rs[c] = rs[c] - factor[:, :right.shape[1]] * rrow
    return jnp.concatenate([r * lax.rsqrt(d) for r, d in zip(rs, diag)], axis=0)


def kernel(rows, cols, subs, assets,
           returns_ref, starts_ref, start_ref, out_ref,
           held, begins, firsts, obuf, xbuf, sbuf, part, rs, mine, quad, mloc, mall,
           ls, bs, os, xs, xr, to_right, to_left, sr, ps, pr, qs, qr, ms, mr):
    r = lax.axis_index("rows")
    mates = cols * subs
    m = lax.axis_index("cols") * subs + lax.axis_index("sub")
    windows, days, width = returns_ref.shape
    k = start_ref.shape[1]
    total = days * rows
    own = width // rows
    half = (k + total) // 2

    def row_peer(d):
        return lax.rem(r + d, rows)

    def mate(d):
        return lax.rem(m + d, mates)

    def row_id(q):
        return {"rows": q}

    def mate_id(q):
        return {"cols": q // subs, "sub": lax.rem(q, subs)}

    def columns(q):
        return pl.ds(pl.multiple_of(q * own, own), own)

    loads = [pltpu.make_async_copy(returns_ref.at[w], held.at[w], ls.at[w]) for w in range(windows)]
    for c in loads:
        c.start()
    load_begins = pltpu.make_async_copy(starts_ref.at[:, columns(r)], begins, bs.at[0])
    load_begins.start()
    load_firsts = pltpu.make_async_copy(start_ref.at[:, :, columns(r)], firsts, bs.at[1])
    load_firsts.start()

    barrier = pltpu.get_barrier_semaphore()
    for d in range(1, rows):
        pl.semaphore_signal(barrier, inc=1, device_id=row_id(row_peer(d)), device_id_type=MESH)
    for d in range(1, mates):
        pl.semaphore_signal(barrier, inc=1, device_id=mate_id(mate(d)), device_id_type=MESH)
    pl.semaphore_wait(barrier, rows - 1 + mates - 1)

    def copy_to(src, dst, send, recv, target):
        return pltpu.make_async_remote_copy(
            src_ref=src, dst_ref=dst, send_sem=send, recv_sem=recv,
            device_id=target, device_id_type=MESH)

    sends = []
    for w in range(windows):
        loads[w].wait()
        for d in range(1, rows):
            q = row_peer(d)
            c = copy_to(held.at[w, :, columns(q)], xbuf.at[r, w], xs.at[w, d],
                        xr.at[w, r], row_id(q))
            c.start()
            sends.append(c)
    xbuf[r] = held[:, :, columns(r)]
    load_begins.wait()
    load_firsts.wait()

    def hop(q, w, right):
        sem = to_right if right else to_left
        target = row_id(lax.rem(r + (1 if right else rows - 1), rows))
        return copy_to(sbuf.at[q, w], sbuf.at[q, w], sem.at[q, w], sr.at[q, w], target)

    def hops(t, some, act):
        right_block = lax.rem(r - t + rows, rows)
        left_block = lax.rem(r + t, rows)
        for w in some:
            @pl.when(jnp.logical_and(r - t >= 0, r < rows - 1))
            def _():
                act(hop(right_block, w, True), t > 0)

            @pl.when(jnp.logical_and(r + t < rows, r > 0))
            def _():
                act(hop(left_block, w, False), t > 0)

    def forward(t, some):
        for w in some:
            if t > 0:
                @pl.when(r - t >= 0)
                def _():
                    hop(lax.rem(r - t + rows, rows), w, True).wait_recv()

                @pl.when(r + t < rows)
                def _():
                    hop(lax.rem(r + t, rows), w, True).wait_recv()
            hops(t, (w,), lambda c, _: c.start())

    def deliver(w):
        return copy_to(part.at[w], rs.at[r], ps.at[w], pr.at[r], row_id(w))

    ahead = windows // 2
    day = lax.broadcasted_iota(jnp.int32, (total, own), 0)
    for w in range(windows):
        for d in range(1, rows):
            q = row_peer(d)
            copy_to(held.at[w, :, columns(q)], xbuf.at[q, w], xs.at[w, d],
                    xr.at[w, q], row_id(q)).wait_recv()
        x = jnp.concatenate([xbuf[q, w] for q in range(rows)], axis=0)
        begin = begins[w:w + 1]
        live = day >= begin
        counts = (total - begin).astype(jnp.float32)
        mean = jnp.sum(jnp.where(live, x, 0.0), axis=0, keepdims=True) / counts
        centered = jnp.where(live, x - mean, 0.0)
        squares = jnp.sum(centered * centered, axis=0, keepdims=True)
        scaled = (centered * lax.rsqrt(squares + 1.0)).astype(jnp.bfloat16)
        sbuf[r, w] = scaled
        first = firsts[w].astype(jnp.bfloat16)
        sums = lax.dot_general(jnp.concatenate([first, scaled], axis=0), scaled, NT,
                               preferred_element_type=jnp.float32)
        part[w] = jnp.concatenate([sums[:half], sums[half:]], axis=1)

        @pl.when(r != w)
        def _():
            deliver(w).start()

        if w < ahead:
            forward(0, (w,))


    early, late = range(windows // 2), range(windows // 2, windows)
    schedule = [(t, some) for t in range(1, rows) for some in (early, late)]
    forward(0, range(ahead, windows))
    rs[r] = part[r]
    for d in range(1, rows):
        q = row_peer(d)
        copy_to(part.at[q], rs.at[q], ps.at[q], pr.at[q], row_id(q)).wait_recv()
    forward(*schedule.pop(0))
    summed = rs[0]
    for q in range(1, rows):
        summed = summed + rs[q]
    mine[...] = summed
    for d in range(1, mates):
        q = mate(d)
        c = copy_to(mine, quad.at[m], qs.at[d], qr.at[m], mate_id(q))
        c.start()
        sends.append(c)
    quad[m] = summed
    for d in range(1, mates):
        q = mate(d)
        copy_to(mine, quad.at[q], qs.at[d], qr.at[q], mate_id(q)).wait_recv()
    forward(*schedule.pop(0))
    both = quad[0]
    for q in range(1, mates):
        both = both + quad[q]
    both = jnp.concatenate([both[:, :total], both[:, total:]], axis=0)
    proj, corr = both[:k], both[k:]
    for step in range(ITERS):
        if step > 0 and len(schedule) > 2:
            forward(*schedule.pop(0))
        image = jnp.dot(proj, corr, precision=HIGHEST, preferred_element_type=jnp.float32)
        gram = lax.dot_general(image, proj, NT, precision=HIGHEST,
                               preferred_element_type=jnp.float32) / assets
        proj = eliminate(gram, image if step < ITERS - 1 else proj)
    mloc[...] = proj
    for d in range(1, rows):
        q = row_peer(d)
        c = copy_to(mloc, mall.at[r], ms.at[d], mr.at[r], row_id(q))
        c.start()
        sends.append(c)
    mall[r] = proj
    for entry in schedule:
        forward(*entry)
    for d in range(1, rows):
        q = row_peer(d)
        copy_to(mloc, mall.at[q], ms.at[d], mr.at[q], row_id(q)).wait_recv()
    stacked = []
    for w in range(windows):
        value = mall[w]
        high = value.astype(jnp.bfloat16)
        low = (value - high.astype(jnp.float32)).astype(jnp.bfloat16)
        stacked.append(jnp.concatenate([high, low], axis=0))

    def finish(q):
        for w in range(windows):
            wide = jnp.dot(stacked[w], sbuf[q, w], preferred_element_type=jnp.float32)
            obuf[q, w] = wide[:k] + wide[k:]
        c = pltpu.make_async_copy(obuf.at[q], out_ref.at[:, :, columns(q)], os.at[q])
        c.start()

    finish(r)
    for t in range(1, rows):
        for near in (True, False):
            @pl.when(r - t >= 0 if near else r + t < rows)
            def _():
                q = lax.rem(r - t + rows if near else r + t, rows)
                finish(q)
    for c in sends:
        c.wait_send()
    for w in range(windows):
        @pl.when(r != w)
        def _():
            deliver(w).wait_send()
    for t in range(rows):
        hops(t, range(windows), lambda c, _: c.wait_send())
    for q in range(rows):
        pltpu.make_async_copy(obuf.at[q], out_ref.at[:, :, columns(q)], os.at[q]).wait()


def fused(returns, starts, start_block, rows, cols, subs):
    windows, days, width = returns.shape
    k = start_block.shape[1]
    total = days * rows
    own = width // rows
    mates = cols * subs
    half = (k + total) // 2
    f32 = jnp.float32
    dma = pltpu.SemaphoreType.DMA
    return pl.pallas_call(
        functools.partial(kernel, rows, cols, subs, width * mates),
        out_shape=jax.ShapeDtypeStruct(start_block.shape, f32),
        in_specs=[pl.BlockSpec(memory_space=pl.ANY)] * 3,
        out_specs=pl.BlockSpec(memory_space=pl.ANY),
        scratch_shapes=[
            pltpu.VMEM(returns.shape, f32),
            pltpu.VMEM((windows, own), jnp.int32),
            pltpu.VMEM((windows, k, own), f32),
            pltpu.VMEM((rows, windows, k, own), f32),
            pltpu.VMEM((rows, windows, days, own), f32),
            pltpu.VMEM((rows, windows, total, own), jnp.bfloat16),
            pltpu.VMEM((windows, half, 2 * total), f32),
            pltpu.VMEM((rows, half, 2 * total), f32),
            pltpu.VMEM((half, 2 * total), f32),
            pltpu.VMEM((mates, half, 2 * total), f32),
            pltpu.VMEM((k, total), f32),
            pltpu.VMEM((windows, k, total), f32),
            dma((windows,)), dma((2,)), dma((rows,)),
            dma((windows, rows)), dma((windows, rows)),
            dma((rows, windows)), dma((rows, windows)), dma((rows, windows)),
            dma((rows,)), dma((rows,)),
            dma((mates,)), dma((mates,)),
            dma((rows,)), dma((rows,)),
        ],
        compiler_params=pltpu.CompilerParams(collective_id=0, has_side_effects=True),
    )(returns, starts, start_block)


def gram_of(image):
    return jnp.einsum("wkj,wlj->wkl", image, image, precision=HIGHEST)


def project(factors, scaled):
    rounded = factors.astype(jnp.bfloat16)
    return jnp.einsum("wka,wta->wkt", rounded, scaled, preferred_element_type=jnp.float32)


def expand(proj, widened):
    return jnp.einsum("wkt,wta->wka", proj, widened, precision=HIGHEST)


def orthonormal(image, gram, assets):
    lower = jnp.linalg.cholesky(gram / assets)
    return jax.scipy.linalg.solve_triangular(lower, image, lower=True)


def stepwise(returns, starts, start_block, rows, mates):
    windows, days, width = returns.shape
    row_pos = lax.axis_index("rows")
    total_days = days * rows
    day_index = row_pos * days + jnp.arange(days, dtype=jnp.int32)
    live = (day_index[None, :, None] >= starts[:, None, :]).astype(jnp.float32)
    counts = (total_days - starts).astype(jnp.float32)
    masked = live * returns
    sums = lax.psum(jnp.sum(masked, axis=1), "rows")
    mean = sums / counts
    centered = live * (returns - mean[:, None, :])
    squares = lax.psum(jnp.sum(centered * centered, axis=1), "rows")
    scaled = (centered * lax.rsqrt(squares + 1.0)[:, None, :]).astype(jnp.bfloat16)
    widened = scaled.astype(jnp.float32)
    factors = start_block
    for step in range(ITERS):
        proj = lax.psum(project(factors, scaled), ("cols", "sub"))
        image = lax.psum(expand(proj, widened), "rows")
        gram = lax.psum(gram_of(image), ("cols", "sub"))
        factors = orthonormal(image, gram, width * mates)
    return factors


def on_device(rows, cols, subs, returns, starts, start_block):
    windows, days, width = returns.shape
    k = start_block.shape[1]
    fits = (windows == rows and width % (128 * rows) == 0 and days % 8 == 0 and k % 16 == 0
            and days * rows <= 64 and (days * rows + k) % 16 == 0 and rows > 1 and cols * subs > 1)
    if fits:
        return fused(returns, starts, start_block, rows, cols, subs)
    return stepwise(returns, starts, start_block, rows, cols * subs)


def solution(mesh):
    placed = (
        P("groups", "rows", ("cols", "sub")),
        P("groups", ("cols", "sub")),
        P("groups", None, ("cols", "sub")),
    )
    sizes = (mesh.shape["rows"], mesh.shape["cols"], mesh.shape["sub"])
    return jax.shard_map(
        functools.partial(on_device, *sizes),
        mesh=mesh,
        in_specs=placed,
        out_specs=P("groups", None, ("cols", "sub")),
        check_vma=False,
    )
```

profile of v0, /device:TPU:0, one launch (start us, length us, event | category | flops | bytes accessed | tf_op | source)
XLA Modules:
  0.0 42.3 jit_solution(4762233954004428896)
XLA Ops:
  0.0 40.0 %shard_map.37 = f32[4,32,2048]{2,1,0:T(8,128)} custom-call(f32[4,16,2048]{2,1,0:T(8,128)} %returns_ref.1, s32[4,2048]{1,0:T(4,128)} %starts_ref.1, f32[4,32,2048]{2,1,0:T(8,128)} %start_ref.1), custom_call_target="tpu_custom_call" | custom-call | tf_op jit(solution)/shard_map/pallas_call | solution.py:259
  40.1 2.3 %copy.5 = f32[4,32,2048]{2,1,0:T(8,128)} copy(f32[4,32,2048]{2,1,0:T(8,128)} %shard_map.37) | data formatting | bytes 2097152
where the time goes:
time: 42.5 us; the launch traced here: 42.3 us
  Pallas kernels  40 us (94%)
  local copies, waits for them, and re-layouts  2.3 us (5%)
    pallas_call x1, Pallas kernels, fused(): pl.pallas_call(functools.partial(kernel, rows, cols, subs, width * mates)...  40 us
    unnamed x1, local copies, waits for them, and re-layouts  2.3 us

commit v1 on v0

v1 whole, which is shorter than its diff:
```python
import functools

import jax
import jax.numpy as jnp
from jax import lax
from jax.experimental import pallas as pl
from jax.experimental.pallas import tpu as pltpu
from jax.sharding import PartitionSpec as P

ITERS = 3
HIGHEST = lax.Precision.HIGHEST
MESH = pl.DeviceIdType.MESH
NT = (((1,), (1,)), ((), ()))
SUBLANES = 8
LANES = 128
LIMIT = 6.0
TOP = 32767.0
COARSE = 32000.0


def eliminate(gram, right):
    size = gram.shape[0]
    height = min(SUBLANES, size)
    blocks = size // height
    gs = [gram[b * height:(b + 1) * height] for b in range(blocks)]
    rs = [right[b * height:(b + 1) * height] for b in range(blocks)]
    row_id = lax.broadcasted_iota(jnp.int32, (height, 1), 0)
    diag = [jnp.ones((height, right.shape[1]), jnp.float32) for _ in range(blocks)]
    wide = max(size, right.shape[1])
    for b in range(blocks):
        panel = {
            (c, i): jnp.broadcast_to(gs[c][:, b * height + i:b * height + i + 1], (height, wide))
            for c in range(b, blocks) for i in range(height)
        }
        for i in range(height):
            grow = gs[b][i:i + 1]
            rrow = rs[b][i:i + 1]
            pivot = panel[b, i][i:i + 1]
            diag[b] = jnp.where(row_id == i, pivot[:, :right.shape[1]], diag[b])
            inverse = 1.0 / pivot
            ahead = {n: panel[b, n][i:i + 1] for n in range(i + 1, height)}
            for c in range(b, blocks):
                factor = panel[c, i] * inverse
                if c == b:
                    factor = jnp.where(row_id > i, factor, 0.0)
                for n in range(i + 1, height):
                    panel[c, n] = panel[c, n] - factor * ahead[n]
                gs[c] = gs[c] - factor[:, :size] * grow
                rs[c] = rs[c] - factor[:, :right.shape[1]] * rrow
    return jnp.concatenate([r * lax.rsqrt(d) for r, d in zip(rs, diag)], axis=0)


def kernel(rows, cols, subs, assets,
           returns_ref, starts_ref, start_ref, out_ref,
           held, begins, firsts, codes, lhs, sbuf, mine, quad, mloc, mall,
           ls, bs, cs, cr, qs, qr, ms, mr):
    r = lax.axis_index("rows")
    mates = cols * subs
    m = lax.axis_index("cols") * subs + lax.axis_index("sub")
    windows, days, width = returns_ref.shape
    k = start_ref.shape[1]
    total = days * rows
    groups = width // LANES
    half = (k + total) // 2
    ends = ((0, 1), (rows - 1, rows - 2))

    def row_peer(d):
        return lax.rem(r + d, rows)

    def mate(d):
        return lax.rem(m + d, mates)

    def row_id(q):
        return {"rows": q}

    def mate_id(q):
        return {"cols": q // subs, "sub": lax.rem(q, subs)}

    def lanes(g):
        return slice(g * LANES, (g + 1) * LANES)

    load_begins = [pltpu.make_async_copy(starts_ref.at[pl.ds(w, 1)], begins.at[w], bs.at[w]) for w in range(windows)]
    for c in load_begins:
        c.start()
    loads = [pltpu.make_async_copy(returns_ref.at[w], held.at[w], ls.at[w]) for w in range(windows)]
    for c in loads:
        c.start()
    load_firsts = pltpu.make_async_copy(start_ref.at[r], firsts, bs.at[windows])
    load_firsts.start()

    barrier = pltpu.get_barrier_semaphore()
    for d in range(1, rows):
        pl.semaphore_signal(barrier, inc=1, device_id=row_id(row_peer(d)), device_id_type=MESH)
    for d in range(1, mates):
        pl.semaphore_signal(barrier, inc=1, device_id=mate_id(mate(d)), device_id_type=MESH)

    row = lax.broadcasted_iota(jnp.int32, (groups, LANES), 0)
    own_day = r * days + lax.broadcasted_iota(jnp.int32, (days, LANES), 0)
    for w in range(windows):
        load_begins[w].wait()
        loads[w].wait()
        centers = jnp.zeros((groups, LANES), jnp.float32)
        scales = jnp.zeros((groups, LANES), jnp.float32)
        for g in range(groups):
            x = held[w, :, lanes(g)]
            x = jnp.where(own_day >= begins[w, :, lanes(g)], x, x[days - 1:days])
            top = jnp.max(x, axis=0, keepdims=True)
            low = jnp.min(x, axis=0, keepdims=True)
            center = jnp.round((top + low) * (0.5 * TOP / LIMIT))
            middle = center * (LIMIT / TOP)
            reach = jnp.maximum(top - middle, middle - low)
            scale = jnp.floor(reach * (COARSE / LIMIT)) + 1.0
            inverse = (TOP * COARSE / LIMIT) / scale
            codes[r, w, g] = jnp.round((x - middle) * inverse).astype(jnp.int32).astype(jnp.int16)
            centers = jnp.where(row == g, center, centers)
            scales = jnp.where(row == g, scale, scales)
        codes[r, w, groups] = centers.astype(jnp.int32).astype(jnp.int16)
        codes[r, w, groups + 1] = scales.astype(jnp.int32).astype(jnp.int16)

    def unit(s, w, q):
        return pltpu.make_async_remote_copy(
            src_ref=codes.at[s, w], dst_ref=codes.at[s, w], send_sem=cs.at[s, w, q],
            recv_sem=cr.at[s, w], device_id=row_id(q), device_id_type=MESH)

    def sides(t, act):
        for sign in (1, -1):
            q = r + sign * t

            @pl.when(jnp.logical_and(q >= 0, q < rows))
            def _():
                act(q)

    def own_units(act):
        for t in range(rows - 1, 0, -1):
            sides(t, lambda q: act(r, q, q))

        def rest(q, t):
            far = jnp.where(q > r, rows - 1, 0)

            @pl.when(jnp.logical_or(t == 1, jnp.logical_and(q > 0, q < rows - 1)))
            def _():
                for d in range(windows):
                    w = lax.rem(far + 1 + d, windows)

                    @pl.when(w != q)
                    def _():
                        act(r, w, q)

        for t in range(rows - 1, 0, -1):
            sides(t, lambda q: rest(q, t))

    def relayed(e, own):
        near = 1 if e == 0 else rows - 2
        pairs = [(s, w) for w in range(windows) if w != e
                 for s in range(rows) if s not in (e, near)]
        return [p for p in pairs if (p[1] == near) == own]

    def forward(part, parts):
        for e, near in ends:
            @pl.when(r == near)
            def _():
                pairs = relayed(e, False)
                for s, w in pairs[part * len(pairs) // parts:(part + 1) * len(pairs) // parts]:
                    unit(s, w, e).wait_recv()
                    unit(s, w, e).start()

    def relays(s, w):
        flags = [jnp.logical_and(r == near, jnp.logical_and(s != e, w != e)) for e, near in ends]
        return functools.reduce(jnp.logical_or, flags)

    pl.semaphore_wait(barrier, rows - 1 + mates - 1)
    own_units(lambda s, w, q: unit(s, w, q).start())

    load_firsts.wait()
    lhs[:k] = firsts[...].astype(jnp.bfloat16)

    day = lax.broadcasted_iota(jnp.int32, (total, LANES), 0)

    def standardize(w, store):
        middles, steps = [], []
        for s in range(rows):
            middles.append(codes[s, w, groups].astype(jnp.float32) * (LIMIT / TOP))
            steps.append(codes[s, w, groups + 1].astype(jnp.float32) * (LIMIT / TOP / COARSE))
        for g in range(groups):
            x = jnp.concatenate([
                codes[s, w, g].astype(jnp.float32) * steps[s][g:g + 1] + middles[s][g:g + 1]
                for s in range(rows)], axis=0)
            begin = begins[w, :, lanes(g)]
            live = day >= begin
            counts = (total - begin).astype(jnp.float32)
            mean = jnp.sum(jnp.where(live, x, 0.0), axis=0, keepdims=True) / counts
            centered = jnp.where(live, x - mean, 0.0)
            squares = jnp.sum(centered * centered, axis=0, keepdims=True)
            store(g, (centered * lax.rsqrt(squares + 1.0)).astype(jnp.bfloat16))

    for d in range(1, rows):
        unit(row_peer(d), r, r).wait_recv()
    for e, near in ends:
        @pl.when(r == near)
        def _():
            for s, w in relayed(e, True):
                unit(s, w, e).start()

    def keep_own(g, value):
        lhs[k:, lanes(g)] = value

    standardize(r, keep_own)
    sums = lax.dot_general(lhs[...], lhs[k:], NT, preferred_element_type=jnp.float32)
    summed = jnp.concatenate([sums[:half], sums[half:]], axis=1)
    mine[...] = summed
    sends = []
    for d in range(1, mates):
        q = mate(d)
        c = pltpu.make_async_remote_copy(
            src_ref=mine, dst_ref=quad.at[m], send_sem=qs.at[d], recv_sem=qr.at[m],
            device_id=mate_id(q), device_id_type=MESH)
        c.start()
        sends.append(c)
    quad[m] = summed
    forward(0, 2)
    for d in range(1, mates):
        q = mate(d)
        pltpu.make_async_remote_copy(
            src_ref=mine, dst_ref=quad.at[q], send_sem=qs.at[d], recv_sem=qr.at[q],
            device_id=mate_id(q), device_id_type=MESH).wait_recv()
    both = quad[0]
    for q in range(1, mates):
        both = both + quad[q]
    both = jnp.concatenate([both[:, :total], both[:, total:]], axis=0)
    proj, corr = both[:k], both[k:]
    for step in range(ITERS):
        image = jnp.dot(proj, corr, precision=HIGHEST, preferred_element_type=jnp.float32)
        gram = lax.dot_general(image, proj, NT, precision=HIGHEST,
                               preferred_element_type=jnp.float32) / assets
        proj = eliminate(gram, image if step < ITERS - 1 else proj)
        if step == 0:
            forward(1, 2)
    mloc[...] = proj
    mall[r] = proj

    def deliver(q, slot):
        return pltpu.make_async_remote_copy(
            src_ref=mloc, dst_ref=mall.at[slot], send_sem=ms.at[q], recv_sem=mr.at[slot],
            device_id=row_id(q), device_id_type=MESH)

    for t in range(rows - 1, 0, -1):
        sides(t, lambda q: deliver(q, r).start())

    def finish(w, scaled):
        value = mall[w]
        high = value.astype(jnp.bfloat16)
        low = (value - high.astype(jnp.float32)).astype(jnp.bfloat16)
        wide = jnp.dot(jnp.concatenate([high, low], axis=0), scaled,
                       preferred_element_type=jnp.float32)
        out_ref[w] = wide[:k] + wide[k:]

    finish(r, lhs[k:])
    for d in range(1, rows):
        w = row_peer(d)
        for b in range(1, rows):
            s = row_peer(b)

            @pl.when(jnp.logical_not(relays(s, w)))
            def _():
                unit(s, w, r).wait_recv()

        def keep(g, value):
            sbuf[w, :, lanes(g)] = value

        standardize(w, keep)
    for d in range(1, rows):
        w = row_peer(d)
        deliver(w, w).wait_recv()
        finish(w, sbuf[w])
    for c in sends:
        c.wait_send()
    own_units(lambda s, w, q: unit(s, w, q).wait_send())
    for e, near in ends:
        @pl.when(r == near)
        def _():
            for s, w in relayed(e, True) + relayed(e, False):
                unit(s, w, e).wait_send()
    for t in range(rows - 1, 0, -1):
        sides(t, lambda q: deliver(q, r).wait_send())


def fused(returns, starts, start_block, rows, cols, subs):
    windows, days, width = returns.shape
    k = start_block.shape[1]
    total = days * rows
    mates = cols * subs
    half = (k + total) // 2
    groups = width // LANES
    f32, bf16 = jnp.float32, jnp.bfloat16
    dma = pltpu.SemaphoreType.DMA
    return pl.pallas_call(
        functools.partial(kernel, rows, cols, subs, width * mates),
        out_shape=pltpu.VMEM(start_block.shape, f32),
        in_specs=[pl.BlockSpec(memory_space=pl.ANY)] * 3,
        out_specs=pl.BlockSpec(memory_space=pltpu.VMEM),
        scratch_shapes=[
            pltpu.VMEM(returns.shape, f32),
            pltpu.VMEM((windows, 1, width), jnp.int32),
            pltpu.VMEM((k, width), f32),
            pltpu.VMEM((rows, windows, groups + 2, days, LANES), jnp.int16),
            pltpu.VMEM((k + total, width), bf16),
            pltpu.VMEM((windows, total, width), bf16),
            pltpu.VMEM((half, 2 * total), f32),
            pltpu.VMEM((mates, half, 2 * total), f32),
            pltpu.VMEM((k, total), f32),
            pltpu.VMEM((windows, k, total), f32),
            dma((windows,)), dma((windows + 1,)),
            dma((rows, windows, rows)), dma((rows, windows)),
            dma((mates,)), dma((mates,)),
            dma((rows,)), dma((rows,)),
        ],
        compiler_params=pltpu.CompilerParams(collective_id=0, has_side_effects=True),
    )(returns, starts, start_block)


def gram_of(image):
    return jnp.einsum("wkj,wlj->wkl", image, image, precision=HIGHEST)


def project(factors, scaled):
    rounded = factors.astype(jnp.bfloat16)
    return jnp.einsum("wka,wta->wkt", rounded, scaled, preferred_element_type=jnp.float32)


def expand(proj, widened):
    return jnp.einsum("wkt,wta->wka", proj, widened, precision=HIGHEST)


def orthonormal(image, gram, assets):
    lower = jnp.linalg.cholesky(gram / assets)
    return jax.scipy.linalg.solve_triangular(lower, image, lower=True)


def stepwise(returns, starts, start_block, rows, mates):
    windows, days, width = returns.shape
    row_pos = lax.axis_index("rows")
    total_days = days * rows
    day_index = row_pos * days + jnp.arange(days, dtype=jnp.int32)
    live = (day_index[None, :, None] >= starts[:, None, :]).astype(jnp.float32)
    counts = (total_days - starts).astype(jnp.float32)
    masked = live * returns
    sums = lax.psum(jnp.sum(masked, axis=1), "rows")
    mean = sums / counts
    centered = live * (returns - mean[:, None, :])
    squares = lax.psum(jnp.sum(centered * centered, axis=1), "rows")
    scaled = (centered * lax.rsqrt(squares + 1.0)[:, None, :]).astype(jnp.bfloat16)
    widened = scaled.astype(jnp.float32)
    factors = start_block
    for step in range(ITERS):
        proj = lax.psum(project(factors, scaled), ("cols", "sub"))
        image = lax.psum(expand(proj, widened), "rows")
        gram = lax.psum(gram_of(image), ("cols", "sub"))
        factors = orthonormal(image, gram, width * mates)
    return factors


def on_device(rows, cols, subs, returns, starts, start_block):
    windows, days, width = returns.shape
    k = start_block.shape[1]
    fits = (windows == rows and width == LANES * days and days % 16 == 0 and k % 16 == 0
            and days * rows <= 64 and (days * rows + k) % 16 == 0 and rows > 3 and cols * subs > 1)
    if fits:
        return fused(returns, starts, start_block, rows, cols, subs)
    return stepwise(returns, starts, start_block, rows, cols * subs)


def solution(mesh):
    placed = (
        P("groups", "rows", ("cols", "sub")),
        P("groups", ("cols", "sub")),
        P("groups", None, ("cols", "sub")),
    )
    sizes = (mesh.shape["rows"], mesh.shape["cols"], mesh.shape["sub"])
    return jax.shard_map(
        functools.partial(on_device, *sizes),
        mesh=mesh,
        in_specs=placed,
        out_specs=P("groups", None, ("cols", "sub")),
        check_vma=False,
    )
```

time: 42.5 us -> 32.3 us (0.76)
  Pallas kernels: 40 us -> 31.2 us
  local copies, waits for them, and re-layouts: 2.3 us -> 0.97 us
    pallas_call x1, Pallas kernels: 40 us -> 31.2 us  [fused(): pl.pallas_call(functools.partial(kernel, rows, cols, subs, width * mates)...]
    unnamed x1, local copies, waits for them, and re-layouts: 2.3 us -> 0.97 us
where the time goes in v1:
time: 32.3 us; the launch traced here: 32.2 us
  Pallas kernels  31.2 us (97%)
  local copies, waits for them, and re-layouts  0.97 us (3%)
    pallas_call x1, Pallas kernels, fused(): pl.pallas_call(functools.partial(kernel, rows, cols, subs, width * mates)...  31.2 us
    unnamed x1, local copies, waits for them, and re-layouts  0.97 us

profile of v1, /device:TPU:0, one launch (start us, length us, event | category | flops | bytes accessed | tf_op | source)
XLA Modules:
  0.0 32.2 jit_solution(10115388234180902735)
XLA Ops:
  0.0 31.2 %shard_map.37 = f32[4,32,2048]{2,1,0:T(8,128)S(1)} custom-call(f32[4,16,2048]{2,1,0:T(8,128)} %returns_ref.1, s32[4,2048]{1,0:T(4,128)} %starts_ref.1, f32[4,32,2048]{2,1,0:T(8,128)} %start_ref.1), custom_call_target="tpu_custom_call" | custom-call | tf_op jit(solution)/shard_map/pallas_call | solution.py:296
  31.2 1.0 %copy.5 = f32[4,32,2048]{2,1,0:T(8,128)} copy(f32[4,32,2048]{2,1,0:T(8,128)S(1)} %shard_map.37) | data formatting | bytes 2097152

commit v2 on v1

--- a/solution.py
+++ b/solution.py
@@ -15,7 +15,8 @@
 LANES = 128
 LIMIT = 6.0
 TOP = 32767.0
-COARSE = 32000.0
+TINY = 1e-30
+EARLY = 3
 
 
 def eliminate(gram, right):
@@ -52,8 +53,8 @@
 
 def kernel(rows, cols, subs, assets,
            returns_ref, starts_ref, start_ref, out_ref,
-           held, begins, firsts, codes, lhs, sbuf, mine, quad, mloc, mall,
-           ls, bs, cs, cr, qs, qr, ms, mr):
+           held, begins, firsts, codes, lhs, sbuf, mine, quad, mloc, mall, gains,
+           ls, bs, cs, cr, qs, qr, ms, mr, gs, gr, clear):
     r = lax.axis_index("rows")
     mates = cols * subs
     m = lax.axis_index("cols") * subs + lax.axis_index("sub")
@@ -79,10 +80,11 @@
     def lanes(g):
         return slice(g * LANES, (g + 1) * LANES)
 
+    order = [row_peer(d) for d in sorted(range(rows), key=lambda d: -min(d, rows - d))]
     load_begins = [pltpu.make_async_copy(starts_ref.at[pl.ds(w, 1)], begins.at[w], bs.at[w]) for w in range(windows)]
     for c in load_begins:
         c.start()
-    loads = [pltpu.make_async_copy(returns_ref.at[w], held.at[w], ls.at[w]) for w in range(windows)]
+    loads = [pltpu.make_async_copy(returns_ref.at[w], held.at[w], ls.at[w]) for w in order]
     for c in loads:
         c.start()
     load_firsts = pltpu.make_async_copy(start_ref.at[r], firsts, bs.at[windows])
@@ -94,33 +96,41 @@
     for d in range(1, mates):
         pl.semaphore_signal(barrier, inc=1, device_id=mate_id(mate(d)), device_id_type=MESH)
 
+    def unit(s, w, q):
+        return pltpu.make_async_remote_copy(
+            src_ref=codes.at[s, w], dst_ref=codes.at[s, w], send_sem=cs.at[s, w, q],
+            recv_sem=cr.at[s, w], device_id=row_id(q), device_id_type=MESH)
+
+    def gain(s, q):
+        return pltpu.make_async_remote_copy(
+            src_ref=gains.at[s], dst_ref=gains.at[s], send_sem=gs.at[q],
+            recv_sem=gr.at[s], device_id=row_id(q), device_id_type=MESH)
+
     row = lax.broadcasted_iota(jnp.int32, (groups, LANES), 0)
     own_day = r * days + lax.broadcasted_iota(jnp.int32, (days, LANES), 0)
-    for w in range(windows):
-        load_begins[w].wait()
-        loads[w].wait()
+
+    def encode(w):
+        def load(g):
+            x = held[w, :, lanes(g)]
+            return jnp.where(own_day >= begins[w, :, lanes(g)], x, x[days - 1:days])
+
         centers = jnp.zeros((groups, LANES), jnp.float32)
-        scales = jnp.zeros((groups, LANES), jnp.float32)
+        reach = jnp.full((1, LANES), TINY, jnp.float32)
+        middles = []
         for g in range(groups):
-            x = held[w, :, lanes(g)]
-            x = jnp.where(own_day >= begins[w, :, lanes(g)], x, x[days - 1:days])
+            x = load(g)
             top = jnp.max(x, axis=0, keepdims=True)
             low = jnp.min(x, axis=0, keepdims=True)
             center = jnp.round((top + low) * (0.5 * TOP / LIMIT))
             middle = center * (LIMIT / TOP)
-            reach = jnp.maximum(top - middle, middle - low)
-            scale = jnp.floor(reach * (COARSE / LIMIT)) + 1.0
-            inverse = (TOP * COARSE / LIMIT) / scale
-            codes[r, w, g] = jnp.round((x - middle) * inverse).astype(jnp.int32).astype(jnp.int16)
+            reach = jnp.maximum(reach, jnp.maximum(top - middle, middle - low))
             centers = jnp.where(row == g, center, centers)
-            scales = jnp.where(row == g, scale, scales)
+            middles.append(middle)
         codes[r, w, groups] = centers.astype(jnp.int32).astype(jnp.int16)
-        codes[r, w, groups + 1] = scales.astype(jnp.int32).astype(jnp.int16)
-
-    def unit(s, w, q):
-        return pltpu.make_async_remote_copy(
-            src_ref=codes.at[s, w], dst_ref=codes.at[s, w], send_sem=cs.at[s, w, q],
-            recv_sem=cr.at[s, w], device_id=row_id(q), device_id_type=MESH)
+        gains[r, w] = reach * (1.0 / TOP)
+        inverse = TOP / reach
+        for g in range(groups):
+            codes[r, w, g] = jnp.round((load(g) - middles[g]) * inverse).astype(jnp.int32).astype(jnp.int16)
 
     def sides(t, act):
         for sign in (1, -1):
@@ -130,29 +140,37 @@
             def _():
                 act(q)
 
-    def own_units(act):
+    def other_units(act, stages):
+        def rest(q, t, right):
+            end = jnp.logical_or(q == 0, q == rows - 1)
+            for d in range(windows):
+                w = d if right else windows - 1 - d
+                inner = (1 if d == 0 else 2 if d < windows - 1 else 3) in stages
+                outer = t == 1 and (0 if d < EARLY else 1) in stages
+                if not inner and not outer:
+                    continue
+                take = q != w
+                if not outer:
+                    take = jnp.logical_and(take, jnp.logical_not(end))
+                if not inner:
+                    take = jnp.logical_and(take, end)
+
+                @pl.when(take)
+                def _():
+                    act(r, w, q)
+
         for t in range(rows - 1, 0, -1):
-            sides(t, lambda q: act(r, q, q))
-
-        def rest(q, t):
-            far = jnp.where(q > r, rows - 1, 0)
-
-            @pl.when(jnp.logical_or(t == 1, jnp.logical_and(q > 0, q < rows - 1)))
-            def _():
-                for d in range(windows):
-                    w = lax.rem(far + 1 + d, windows)
-
-                    @pl.when(w != q)
-                    def _():
-                        act(r, w, q)
-
-        for t in range(rows - 1, 0, -1):
-            sides(t, lambda q: rest(q, t))
+            for sign in (1, -1):
+                q = r + sign * t
+
+                @pl.when(jnp.logical_and(q >= 0, q < rows))
+                def _():
+                    rest(q, t, sign > 0)
 
     def relayed(e, own):
         near = 1 if e == 0 else rows - 2
-        pairs = [(s, w) for w in range(windows) if w != e
-                 for s in range(rows) if s not in (e, near)]
+        turn = range(windows) if e else range(windows - 1, -1, -1)
+        pairs = [(s, w) for w in turn if w != e for s in range(rows) if s not in (e, near)]
         return [p for p in pairs if (p[1] == near) == own]
 
     def forward(part, parts):
@@ -168,22 +186,37 @@
         flags = [jnp.logical_and(r == near, jnp.logical_and(s != e, w != e)) for e, near in ends]
         return functools.reduce(jnp.logical_or, flags)
 
-    pl.semaphore_wait(barrier, rows - 1 + mates - 1)
-    own_units(lambda s, w, q: unit(s, w, q).start())
+    for c in load_begins:
+        c.wait()
+    for i, w in enumerate(order):
+        loads[i].wait()
+        encode(w)
+        if i == 1:
+            pl.semaphore_wait(barrier, rows - 1 + mates - 1)
+        if i > 0:
+            unit(r, order[i - 1], order[i - 1]).start()
+    for d in range(1, rows):
+        gain(r, row_peer(d)).start()
+    other_units(lambda s, w, q: unit(s, w, q).start(), (0,))
 
     load_firsts.wait()
     lhs[:k] = firsts[...].astype(jnp.bfloat16)
+    for w in order[:-1]:
+        unit(r, w, w).wait_send()
+    for d in range(1, subs):
+        pl.semaphore_signal(clear, inc=1, device_id={"sub": lax.rem(lax.axis_index("sub") + d, subs)},
+                            device_id_type=MESH)
+    pl.semaphore_wait(clear, subs - 1)
+    other_units(lambda s, w, q: unit(s, w, q).start(), (1,))
 
     day = lax.broadcasted_iota(jnp.int32, (total, LANES), 0)
 
     def standardize(w, store):
-        middles, steps = [], []
-        for s in range(rows):
-            middles.append(codes[s, w, groups].astype(jnp.float32) * (LIMIT / TOP))
-            steps.append(codes[s, w, groups + 1].astype(jnp.float32) * (LIMIT / TOP / COARSE))
+        middles = [codes[s, w, groups].astype(jnp.float32) * (LIMIT / TOP) for s in range(rows)]
+        steps = [gains[s, w] for s in range(rows)]
         for g in range(groups):
             x = jnp.concatenate([
-                codes[s, w, g].astype(jnp.float32) * steps[s][g:g + 1] + middles[s][g:g + 1]
+                codes[s, w, g].astype(jnp.float32) * steps[s] + middles[s][g:g + 1]
                 for s in range(rows)], axis=0)
             begin = begins[w, :, lanes(g)]
             live = day >= begin
@@ -194,6 +227,7 @@
             store(g, (centered * lax.rsqrt(squares + 1.0)).astype(jnp.bfloat16))
 
     for d in range(1, rows):
+        gain(row_peer(d), r).wait_recv()
         unit(row_peer(d), r, r).wait_recv()
     for e, near in ends:
         @pl.when(r == near)
@@ -217,12 +251,14 @@
         c.start()
         sends.append(c)
     quad[m] = summed
-    forward(0, 2)
+    other_units(lambda s, w, q: unit(s, w, q).start(), (2,))
     for d in range(1, mates):
         q = mate(d)
         pltpu.make_async_remote_copy(
             src_ref=mine, dst_ref=quad.at[q], send_sem=qs.at[d], recv_sem=qr.at[q],
             device_id=mate_id(q), device_id_type=MESH).wait_recv()
+    other_units(lambda s, w, q: unit(s, w, q).start(), (3,))
+    forward(0, 2)
     both = quad[0]
     for q in range(1, mates):
         both = both + quad[q]
@@ -233,7 +269,7 @@
         gram = lax.dot_general(image, proj, NT, precision=HIGHEST,
                                preferred_element_type=jnp.float32) / assets
         proj = eliminate(gram, image if step < ITERS - 1 else proj)
-        if step == 0:
+        if step == 1:
             forward(1, 2)
     mloc[...] = proj
     mall[r] = proj
@@ -274,7 +310,9 @@
         finish(w, sbuf[w])
     for c in sends:
         c.wait_send()
-    own_units(lambda s, w, q: unit(s, w, q).wait_send())
+    for d in range(1, rows):
+        gain(r, row_peer(d)).wait_send()
+    other_units(lambda s, w, q: unit(s, w, q).wait_send(), (0, 1, 2, 3))
     for e, near in ends:
         @pl.when(r == near)
         def _():
@@ -302,17 +340,18 @@
             pltpu.VMEM(returns.shape, f32),
             pltpu.VMEM((windows, 1, width), jnp.int32),
             pltpu.VMEM((k, width), f32),
-            pltpu.VMEM((rows, windows, groups + 2, days, LANES), jnp.int16),
+            pltpu.VMEM((rows, windows, groups + 1, days, LANES), jnp.int16),
             pltpu.VMEM((k + total, width), bf16),
             pltpu.VMEM((windows, total, width), bf16),
             pltpu.VMEM((half, 2 * total), f32),
             pltpu.VMEM((mates, half, 2 * total), f32),
             pltpu.VMEM((k, total), f32),
             pltpu.VMEM((windows, k, total), f32),
+            pltpu.VMEM((rows, windows, 1, LANES), f32),
             dma((windows,)), dma((windows + 1,)),
             dma((rows, windows, rows)), dma((rows, windows)),
             dma((mates,)), dma((mates,)),
-            dma((rows,)), dma((rows,)),
+            dma((rows,)), dma((rows,)), dma((rows,)), dma((rows,)), pltpu.SemaphoreType.REGULAR,
         ],
         compiler_params=pltpu.CompilerParams(collective_id=0, has_side_effects=True),
     )(returns, starts, start_block)

time: 32.3 us -> 28.7 us (0.89)
  Pallas kernels: 31.2 us -> 27.6 us
    pallas_call x1, Pallas kernels: 31.2 us -> 27.6 us  [fused(): pl.pallas_call(functools.partial(kernel, rows, cols, subs, width * mates)...]
where the time goes in v2:
time: 28.7 us; the launch traced here: 28.5 us
  Pallas kernels  27.6 us (96%)
  local copies, waits for them, and re-layouts  0.97 us (3%)
    pallas_call x1, Pallas kernels, fused(): pl.pallas_call(functools.partial(kernel, rows, cols, subs, width * mates)...  27.6 us
    unnamed x1, local copies, waits for them, and re-layouts  0.97 us

profile of v2, /device:TPU:0, one launch (start us, length us, event | category | flops | bytes accessed | tf_op | source)
XLA Modules:
  0.0 28.5 jit_solution(4561142332493292501)
XLA Ops:
  0.0 27.6 %shard_map.37 = f32[4,32,2048]{2,1,0:T(8,128)S(1)} custom-call(f32[4,16,2048]{2,1,0:T(8,128)} %returns_ref.1, s32[4,2048]{1,0:T(4,128)} %starts_ref.1, f32[4,32,2048]{2,1,0:T(8,128)} %start_ref.1), custom_call_target="tpu_custom_call" | custom-call | tf_op jit(solution)/shard_map/pallas_call | solution.py:334
  27.6 1.0 %copy.5 = f32[4,32,2048]{2,1,0:T(8,128)} copy(f32[4,32,2048]{2,1,0:T(8,128)S(1)} %shard_map.37) | data formatting | bytes 2097152

commit v3 on v2

--- a/solution.py
+++ b/solution.py
@@ -16,45 +16,70 @@
 LIMIT = 6.0
 TOP = 32767.0
 TINY = 1e-30
-EARLY = 3
-
-
-def eliminate(gram, right):
-    size = gram.shape[0]
-    height = min(SUBLANES, size)
-    blocks = size // height
-    gs = [gram[b * height:(b + 1) * height] for b in range(blocks)]
-    rs = [right[b * height:(b + 1) * height] for b in range(blocks)]
-    row_id = lax.broadcasted_iota(jnp.int32, (height, 1), 0)
-    diag = [jnp.ones((height, right.shape[1]), jnp.float32) for _ in range(blocks)]
-    wide = max(size, right.shape[1])
-    for b in range(blocks):
-        panel = {
-            (c, i): jnp.broadcast_to(gs[c][:, b * height + i:b * height + i + 1], (height, wide))
-            for c in range(b, blocks) for i in range(height)
-        }
-        for i in range(height):
-            grow = gs[b][i:i + 1]
-            rrow = rs[b][i:i + 1]
-            pivot = panel[b, i][i:i + 1]
-            diag[b] = jnp.where(row_id == i, pivot[:, :right.shape[1]], diag[b])
-            inverse = 1.0 / pivot
-            ahead = {n: panel[b, n][i:i + 1] for n in range(i + 1, height)}
-            for c in range(b, blocks):
-                factor = panel[c, i] * inverse
-                if c == b:
-                    factor = jnp.where(row_id > i, factor, 0.0)
-                for n in range(i + 1, height):
+
+
+def eliminate(gram, rights):
+    size, wide = gram.shape[0], rights[0].shape[1]
+    tiles = size // SUBLANES
+    sums = [[x[c * SUBLANES:(c + 1) * SUBLANES] for c in range(tiles)] for x in rights]
+    row_id = lax.broadcasted_iota(jnp.int32, (SUBLANES, 1), 0)
+    diag = [jnp.ones((SUBLANES, wide), jnp.float32) for _ in range(tiles)]
+    panel = {
+        (c, i): jnp.broadcast_to(gram[c * SUBLANES:(c + 1) * SUBLANES, i:i + 1], (SUBLANES, wide))
+        for i in range(size) for c in range(i // SUBLANES, tiles)
+    }
+    for i in range(size):
+        own, sub = i // SUBLANES, i % SUBLANES
+        pivot = panel[own, i][sub:sub + 1]
+        inverse = 1.0 / pivot
+        diag[own] = jnp.where(row_id == sub, pivot, diag[own])
+        ahead = {n: panel[n // SUBLANES, i][n % SUBLANES:n % SUBLANES + 1] for n in range(i + 1, size)}
+        rows = [x[own][sub:sub + 1] for x in sums]
+        for c in range(own, tiles):
+            factor = panel[c, i] * inverse
+            if c == own:
+                factor = jnp.where(row_id > sub, factor, 0.0)
+            for n in range(i + 1, size):
+                if c >= n // SUBLANES:
                     panel[c, n] = panel[c, n] - factor * ahead[n]
-                gs[c] = gs[c] - factor[:, :size] * grow
-                rs[c] = rs[c] - factor[:, :right.shape[1]] * rrow
-    return jnp.concatenate([r * lax.rsqrt(d) for r, d in zip(rs, diag)], axis=0)
+            for x, row in zip(sums, rows):
+                x[c] = x[c] - factor * row
+    roots = [lax.rsqrt(d) for d in diag]
+    return [jnp.concatenate([v * d for v, d in zip(x, roots)], axis=0) for x in sums]
+
+
+def exact(left, right):
+    return jnp.dot(left, right, precision=HIGHEST, preferred_element_type=jnp.float32)
+
+
+def background(rows, windows, x):
+    plan = []
+    for q in range(rows):
+        end = q in (0, rows - 1)
+        if q == x or (end and abs(q - x) > 1):
+            continue
+        for d in range(windows):
+            w = d if q > x else windows - 1 - d
+            if w != q:
+                plan.append((x, w, q, 0 if end else 1 if d == 0 else 3 if d == windows - 1 else 2))
+    for e, near in ((0, 1), (rows - 1, rows - 2)):
+        if x == near:
+            far = [s for s in range(rows) if s not in (e, near)]
+            plan += [(s, near, e, 4) for s in far]
+            turn = [w for w in (range(windows) if e else range(windows - 1, -1, -1)) if w not in (e, near)]
+            plan += [(s, w, e, 5 + i * 2 // len(turn)) for i, w in enumerate(turn) for s in far]
+    return plan
+
+
+def block(count, rows, windows):
+    sides = [(a, count // a) for a in range(1, rows + 1) if count % a == 0 and count // a <= windows]
+    return sides[0] if sides else None
 
 
 def kernel(rows, cols, subs, assets,
            returns_ref, starts_ref, start_ref, out_ref,
-           held, begins, firsts, codes, lhs, sbuf, mine, quad, mloc, mall, gains,
-           ls, bs, cs, cr, qs, qr, ms, mr, gs, gr, clear):
+           held, begins, firsts, codes, lhs, sbuf, mine, quad, mix, gains,
+           ls, bs, cs, cr, qs, qr, ms, mr, gs, gr, rest, clear):
     r = lax.axis_index("rows")
     mates = cols * subs
     m = lax.axis_index("cols") * subs + lax.axis_index("sub")
@@ -96,10 +121,11 @@
     for d in range(1, mates):
         pl.semaphore_signal(barrier, inc=1, device_id=mate_id(mate(d)), device_id_type=MESH)
 
-    def unit(s, w, q):
+    def unit(s, w, q, sem=None):
         return pltpu.make_async_remote_copy(
-            src_ref=codes.at[s, w], dst_ref=codes.at[s, w], send_sem=cs.at[s, w, q],
-            recv_sem=cr.at[s, w], device_id=row_id(q), device_id_type=MESH)
+            src_ref=codes.at[s, w], dst_ref=codes.at[s, w],
+            send_sem=cs.at[w] if sem is None else sem.at[0], recv_sem=cr.at[s, w],
+            device_id=row_id(q), device_id_type=MESH)
 
     def gain(s, q):
         return pltpu.make_async_remote_copy(
@@ -132,57 +158,20 @@
         for g in range(groups):
             codes[r, w, g] = jnp.round((load(g) - middles[g]) * inverse).astype(jnp.int32).astype(jnp.int16)
 
-    def sides(t, act):
-        for sign in (1, -1):
-            q = r + sign * t
-
-            @pl.when(jnp.logical_and(q >= 0, q < rows))
-            def _():
-                act(q)
-
-    def other_units(act, stages):
-        def rest(q, t, right):
-            end = jnp.logical_or(q == 0, q == rows - 1)
-            for d in range(windows):
-                w = d if right else windows - 1 - d
-                inner = (1 if d == 0 else 2 if d < windows - 1 else 3) in stages
-                outer = t == 1 and (0 if d < EARLY else 1) in stages
-                if not inner and not outer:
-                    continue
-                take = q != w
-                if not outer:
-                    take = jnp.logical_and(take, jnp.logical_not(end))
-                if not inner:
-                    take = jnp.logical_and(take, end)
-
-                @pl.when(take)
+    plans = [background(rows, windows, x) for x in range(rows)]
+
+    def stage(number):
+        for x, plan in enumerate(plans):
+            some = [p for p in plan if p[3] == number]
+            if some:
+                @pl.when(r == x)
                 def _():
-                    act(r, w, q)
-
-        for t in range(rows - 1, 0, -1):
-            for sign in (1, -1):
-                q = r + sign * t
-
-                @pl.when(jnp.logical_and(q >= 0, q < rows))
-                def _():
-                    rest(q, t, sign > 0)
-
-    def relayed(e, own):
-        near = 1 if e == 0 else rows - 2
-        turn = range(windows) if e else range(windows - 1, -1, -1)
-        pairs = [(s, w) for w in turn if w != e for s in range(rows) if s not in (e, near)]
-        return [p for p in pairs if (p[1] == near) == own]
-
-    def forward(part, parts):
-        for e, near in ends:
-            @pl.when(r == near)
-            def _():
-                pairs = relayed(e, False)
-                for s, w in pairs[part * len(pairs) // parts:(part + 1) * len(pairs) // parts]:
-                    unit(s, w, e).wait_recv()
-                    unit(s, w, e).start()
-
-    def relays(s, w):
+                    for s, w, q, _ in some:
+                        if number > 4:
+                            unit(s, w, q).wait_recv()
+                        unit(s, w, q, rest).start()
+
+    def relayed(s, w):
         flags = [jnp.logical_and(r == near, jnp.logical_and(s != e, w != e)) for e, near in ends]
         return functools.reduce(jnp.logical_or, flags)
 
@@ -197,7 +186,7 @@
             unit(r, order[i - 1], order[i - 1]).start()
     for d in range(1, rows):
         gain(r, row_peer(d)).start()
-    other_units(lambda s, w, q: unit(s, w, q).start(), (0,))
+    stage(0)
 
     load_firsts.wait()
     lhs[:k] = firsts[...].astype(jnp.bfloat16)
@@ -207,7 +196,7 @@
         pl.semaphore_signal(clear, inc=1, device_id={"sub": lax.rem(lax.axis_index("sub") + d, subs)},
                             device_id_type=MESH)
     pl.semaphore_wait(clear, subs - 1)
-    other_units(lambda s, w, q: unit(s, w, q).start(), (1,))
+    stage(1)
 
     day = lax.broadcasted_iota(jnp.int32, (total, LANES), 0)
 
@@ -229,11 +218,7 @@
     for d in range(1, rows):
         gain(row_peer(d), r).wait_recv()
         unit(row_peer(d), r, r).wait_recv()
-    for e, near in ends:
-        @pl.when(r == near)
-        def _():
-            for s, w in relayed(e, True):
-                unit(s, w, e).start()
+    stage(4)
 
     def keep_own(g, value):
         lhs[k:, lanes(g)] = value
@@ -251,52 +236,57 @@
         c.start()
         sends.append(c)
     quad[m] = summed
-    other_units(lambda s, w, q: unit(s, w, q).start(), (2,))
+    stage(2)
     for d in range(1, mates):
         q = mate(d)
         pltpu.make_async_remote_copy(
             src_ref=mine, dst_ref=quad.at[q], send_sem=qs.at[d], recv_sem=qr.at[q],
             device_id=mate_id(q), device_id_type=MESH).wait_recv()
-    other_units(lambda s, w, q: unit(s, w, q).start(), (3,))
-    forward(0, 2)
+    stage(3)
+    stage(5)
     both = quad[0]
     for q in range(1, mates):
         both = both + quad[q]
     both = jnp.concatenate([both[:, :total], both[:, total:]], axis=0)
     proj, corr = both[:k], both[k:]
+    image = exact(proj, corr)
     for step in range(ITERS):
-        image = jnp.dot(proj, corr, precision=HIGHEST, preferred_element_type=jnp.float32)
         gram = lax.dot_general(image, proj, NT, precision=HIGHEST,
                                preferred_element_type=jnp.float32) / assets
-        proj = eliminate(gram, image if step < ITERS - 1 else proj)
-        if step == 1:
-            forward(1, 2)
-    mloc[...] = proj
-    mall[r] = proj
-
-    def deliver(q, slot):
+        if step < ITERS - 1:
+            proj, image = eliminate(gram, [image, exact(image, corr)])
+        else:
+            proj, = eliminate(gram, [proj])
+    high = proj.astype(jnp.bfloat16)
+    low = (proj - high.astype(jnp.float32)).astype(jnp.bfloat16)
+    mix[r] = jnp.concatenate([high, low], axis=0)
+
+    def deliver(slot, q):
         return pltpu.make_async_remote_copy(
-            src_ref=mloc, dst_ref=mall.at[slot], send_sem=ms.at[q], recv_sem=mr.at[slot],
+            src_ref=mix.at[slot], dst_ref=mix.at[slot], send_sem=ms.at[q], recv_sem=mr.at[slot],
             device_id=row_id(q), device_id_type=MESH)
 
-    for t in range(rows - 1, 0, -1):
-        sides(t, lambda q: deliver(q, r).start())
+    for q in order[:-1]:
+        deliver(r, q).start()
+    stage(6)
 
     def finish(w, scaled):
-        value = mall[w]
-        high = value.astype(jnp.bfloat16)
-        low = (value - high.astype(jnp.float32)).astype(jnp.bfloat16)
-        wide = jnp.dot(jnp.concatenate([high, low], axis=0), scaled,
-                       preferred_element_type=jnp.float32)
+        wide = jnp.dot(mix[w], scaled, preferred_element_type=jnp.float32)
         out_ref[w] = wide[:k] + wide[k:]
 
     finish(r, lhs[k:])
-    for d in range(1, rows):
-        w = row_peer(d)
+    upper = r >= rows // 2
+    mirrored = jnp.where(upper, r, rows - 1 - r)
+    turn = []
+    for j in range(rows - 1):
+        inner = jnp.where(mirrored > j, j, j + 1)
+        w = jnp.where(mirrored == rows - 1, rows - 2 if j == 0 else j - 1, inner)
+        turn.append(jnp.where(upper, w, rows - 1 - w))
+    for w in turn:
         for b in range(1, rows):
             s = row_peer(b)
 
-            @pl.when(jnp.logical_not(relays(s, w)))
+            @pl.when(jnp.logical_not(relayed(s, w)))
             def _():
                 unit(s, w, r).wait_recv()
 
@@ -304,22 +294,26 @@
             sbuf[w, :, lanes(g)] = value
 
         standardize(w, keep)
-    for d in range(1, rows):
-        w = row_peer(d)
+    for w in turn:
         deliver(w, w).wait_recv()
+    for w in turn:
         finish(w, sbuf[w])
     for c in sends:
         c.wait_send()
     for d in range(1, rows):
         gain(r, row_peer(d)).wait_send()
-    other_units(lambda s, w, q: unit(s, w, q).wait_send(), (0, 1, 2, 3))
-    for e, near in ends:
-        @pl.when(r == near)
+    for q in order[:-1]:
+        deliver(r, q).wait_send()
+    for count in sorted({len(plan) for plan in plans}):
+        high, wide = block(count, rows, windows)
+        some = [x for x, plan in enumerate(plans) if len(plan) == count]
+
+        @pl.when(functools.reduce(jnp.logical_or, [r == x for x in some]))
         def _():
-            for s, w in relayed(e, True) + relayed(e, False):
-                unit(s, w, e).wait_send()
-    for t in range(rows - 1, 0, -1):
-        sides(t, lambda q: deliver(q, r).wait_send())
+            whole = codes.at[pl.ds(0, high), pl.ds(0, wide)]
+            pltpu.make_async_remote_copy(
+                src_ref=whole, dst_ref=whole, send_sem=rest.at[0], recv_sem=cr.at[0, 0],
+                device_id=row_id(row_peer(1)), device_id_type=MESH).wait_send()
 
 
 def fused(returns, starts, start_block, rows, cols, subs):
@@ -345,13 +339,12 @@
             pltpu.VMEM((windows, total, width), bf16),
             pltpu.VMEM((half, 2 * total), f32),
             pltpu.VMEM((mates, half, 2 * total), f32),
-            pltpu.VMEM((k, total), f32),
-            pltpu.VMEM((windows, k, total), f32),
+            pltpu.VMEM((windows, 2 * k, total), bf16),
             pltpu.VMEM((rows, windows, 1, LANES), f32),
             dma((windows,)), dma((windows + 1,)),
-            dma((rows, windows, rows)), dma((rows, windows)),
+            dma((windows,)), dma((rows, windows)),
             dma((mates,)), dma((mates,)),
-            dma((rows,)), dma((rows,)), dma((rows,)), dma((rows,)), pltpu.SemaphoreType.REGULAR,
+            dma((rows,)), dma((rows,)), dma((rows,)), dma((rows,)), dma((1,)), pltpu.SemaphoreType.REGULAR,
         ],
         compiler_params=pltpu.CompilerParams(collective_id=0, has_side_effects=True),
     )(returns, starts, start_block)
@@ -402,7 +395,8 @@
     windows, days, width = returns.shape
     k = start_block.shape[1]
     fits = (windows == rows and width == LANES * days and days % 16 == 0 and k % 16 == 0
-            and days * rows <= 64 and (days * rows + k) % 16 == 0 and rows > 3 and cols * subs > 1)
+            and days * rows <= 64 and (days * rows + k) % 16 == 0 and rows > 3 and cols * subs > 1
+            and all(block(len(background(rows, windows, x)), rows, windows) for x in range(rows)))
     if fits:
         return fused(returns, starts, start_block, rows, cols, subs)
     return stepwise(returns, starts, start_block, rows, cols * subs)

time: 28.7 us -> 27.6 us (0.962)
  Pallas kernels: 27.6 us -> 26.5 us
    pallas_call x1, Pallas kernels: 27.6 us -> 26.5 us  [fused(): pl.pallas_call(functools.partial(kernel, rows, cols, subs, width * mates)...]
where the time goes in v3:
time: 27.6 us; the launch traced here: 27.5 us
  Pallas kernels  26.5 us (96%)
  local copies, waits for them, and re-layouts  0.97 us (4%)
    pallas_call x1, Pallas kernels, fused(): pl.pallas_call(functools.partial(kernel, rows, cols, subs, width * mates)...  26.5 us
    unnamed x1, local copies, waits for them, and re-layouts  0.97 us

profile of v3, /device:TPU:0, one launch (start us, length us, event | category | flops | bytes accessed | tf_op | source)
XLA Modules:
  0.0 27.5 jit_solution(6125985481443808697)
XLA Ops:
  0.0 26.5 %shard_map.37 = f32[4,32,2048]{2,1,0:T(8,128)S(1)} custom-call(f32[4,16,2048]{2,1,0:T(8,128)} %returns_ref.1, s32[4,2048]{1,0:T(4,128)} %starts_ref.1, f32[4,32,2048]{2,1,0:T(8,128)} %start_ref.1), custom_call_target="tpu_custom_call" | custom-call | tf_op jit(solution)/shard_map/pallas_call | solution.py:328
  26.5 1.0 %copy.5 = f32[4,32,2048]{2,1,0:T(8,128)} copy(f32[4,32,2048]{2,1,0:T(8,128)S(1)} %shard_map.37) | data formatting | bytes 2097152

commit v4 on v3

--- a/solution.py
+++ b/solution.py
@@ -16,6 +16,7 @@
 LIMIT = 6.0
 TOP = 32767.0
 TINY = 1e-30
+PIECES = 2
 
 
 def eliminate(gram, rights):
@@ -52,34 +53,27 @@
     return jnp.dot(left, right, precision=HIGHEST, preferred_element_type=jnp.float32)
 
 
+def wanted(windows, x):
+    some = [w for w in range(windows) if abs(w - x) > 1]
+    return some if x >= windows // 2 else some[::-1]
+
+
 def background(rows, windows, x):
+    ends = (0, rows - 1)
     plan = []
     for q in range(rows):
-        end = q in (0, rows - 1)
-        if q == x or (end and abs(q - x) > 1):
-            continue
-        for d in range(windows):
-            w = d if q > x else windows - 1 - d
-            if w != q:
-                plan.append((x, w, q, 0 if end else 1 if d == 0 else 3 if d == windows - 1 else 2))
-    for e, near in ((0, 1), (rows - 1, rows - 2)):
-        if x == near:
-            far = [s for s in range(rows) if s not in (e, near)]
-            plan += [(s, near, e, 4) for s in far]
-            turn = [w for w in (range(windows) if e else range(windows - 1, -1, -1)) if w not in (e, near)]
-            plan += [(s, w, e, 5 + i * 2 // len(turn)) for i, w in enumerate(turn) for s in far]
+        for d, w in enumerate(wanted(windows, q) if q != x else []):
+            if abs(q - x) == 1:
+                plan.append((w, q, 0 if q in ends or x in ends else 2))
+            else:
+                plan.append((w, q, 1 if q in ends and d == 0 else 2))
     return plan
-
-
-def block(count, rows, windows):
-    sides = [(a, count // a) for a in range(1, rows + 1) if count % a == 0 and count // a <= windows]
-    return sides[0] if sides else None
 
 
 def kernel(rows, cols, subs, assets,
            returns_ref, starts_ref, start_ref, out_ref,
-           held, begins, firsts, codes, lhs, sbuf, mine, quad, mix, gains,
-           ls, bs, cs, cr, qs, qr, ms, mr, gs, gr, rest, clear):
+           held, begins, firsts, codes, lhs, sbuf, mine, quad, mix, gains, made, got,
+           ls, bs, cs, cr, qs, qr, ms, mr, gs, gr, rest, hs, hr, clear):
     r = lax.axis_index("rows")
     mates = cols * subs
     m = lax.axis_index("cols") * subs + lax.axis_index("sub")
@@ -88,8 +82,6 @@
     total = days * rows
     groups = width // LANES
     half = (k + total) // 2
-    ends = ((0, 1), (rows - 1, rows - 2))
-
     def row_peer(d):
         return lax.rem(r + d, rows)
 
@@ -123,7 +115,7 @@
 
     def unit(s, w, q, sem=None):
         return pltpu.make_async_remote_copy(
-            src_ref=codes.at[s, w], dst_ref=codes.at[s, w],
+            src_ref=codes.at[s * windows + w], dst_ref=codes.at[s * windows + w],
             send_sem=cs.at[w] if sem is None else sem.at[0], recv_sem=cr.at[s, w],
             device_id=row_id(q), device_id_type=MESH)
 
@@ -152,28 +144,27 @@
             reach = jnp.maximum(reach, jnp.maximum(top - middle, middle - low))
             centers = jnp.where(row == g, center, centers)
             middles.append(middle)
-        codes[r, w, groups] = centers.astype(jnp.int32).astype(jnp.int16)
+        codes[r * windows + w, groups] = centers.astype(jnp.int32).astype(jnp.int16)
         gains[r, w] = reach * (1.0 / TOP)
         inverse = TOP / reach
         for g in range(groups):
-            codes[r, w, g] = jnp.round((load(g) - middles[g]) * inverse).astype(jnp.int32).astype(jnp.int16)
+            codes[r * windows + w, g] = jnp.round((load(g) - middles[g]) * inverse).astype(jnp.int32).astype(jnp.int16)
 
     plans = [background(rows, windows, x) for x in range(rows)]
 
+    def per_row(act):
+        for x in range(rows):
+            @pl.when(r == x)
+            def _():
+                act(x)
+
     def stage(number):
-        for x, plan in enumerate(plans):
-            some = [p for p in plan if p[3] == number]
-            if some:
-                @pl.when(r == x)
-                def _():
-                    for s, w, q, _ in some:
-                        if number > 4:
-                            unit(s, w, q).wait_recv()
-                        unit(s, w, q, rest).start()
-
-    def relayed(s, w):
-        flags = [jnp.logical_and(r == near, jnp.logical_and(s != e, w != e)) for e, near in ends]
-        return functools.reduce(jnp.logical_or, flags)
+        def act(x):
+            for w, q, when in plans[x]:
+                if when == number:
+                    unit(x, w, q, rest).start()
+
+        per_row(act)
 
     for c in load_begins:
         c.wait()
@@ -201,11 +192,11 @@
     day = lax.broadcasted_iota(jnp.int32, (total, LANES), 0)
 
     def standardize(w, store):
-        middles = [codes[s, w, groups].astype(jnp.float32) * (LIMIT / TOP) for s in range(rows)]
+        middles = [codes[s * windows + w, groups].astype(jnp.float32) * (LIMIT / TOP) for s in range(rows)]
         steps = [gains[s, w] for s in range(rows)]
         for g in range(groups):
             x = jnp.concatenate([
-                codes[s, w, g].astype(jnp.float32) * steps[s] + middles[s][g:g + 1]
+                codes[s * windows + w, g].astype(jnp.float32) * steps[s] + middles[s][g:g + 1]
                 for s in range(rows)], axis=0)
             begin = begins[w, :, lanes(g)]
             live = day >= begin
@@ -218,8 +209,6 @@
     for d in range(1, rows):
         gain(row_peer(d), r).wait_recv()
         unit(row_peer(d), r, r).wait_recv()
-    stage(4)
-
     def keep_own(g, value):
         lhs[k:, lanes(g)] = value
 
@@ -242,8 +231,6 @@
         pltpu.make_async_remote_copy(
             src_ref=mine, dst_ref=quad.at[q], send_sem=qs.at[d], recv_sem=qr.at[q],
             device_id=mate_id(q), device_id_type=MESH).wait_recv()
-    stage(3)
-    stage(5)
     both = quad[0]
     for q in range(1, mates):
         both = both + quad[q]
@@ -266,54 +253,87 @@
             src_ref=mix.at[slot], dst_ref=mix.at[slot], send_sem=ms.at[q], recv_sem=mr.at[slot],
             device_id=row_id(q), device_id_type=MESH)
 
-    for q in order[:-1]:
-        deliver(r, q).start()
-    stage(6)
-
-    def finish(w, scaled):
+    def spread(x):
+        for q in range(rows):
+            if abs(q - x) > 1:
+                deliver(x, q).start()
+
+    per_row(spread)
+
+    def loadings(w, scaled):
         wide = jnp.dot(mix[w], scaled, preferred_element_type=jnp.float32)
-        out_ref[w] = wide[:k] + wide[k:]
-
-    finish(r, lhs[k:])
-    upper = r >= rows // 2
-    mirrored = jnp.where(upper, r, rows - 1 - r)
-    turn = []
-    for j in range(rows - 1):
-        inner = jnp.where(mirrored > j, j, j + 1)
-        w = jnp.where(mirrored == rows - 1, rows - 2 if j == 0 else j - 1, inner)
-        turn.append(jnp.where(upper, w, rows - 1 - w))
-    for w in turn:
-        for b in range(1, rows):
-            s = row_peer(b)
-
-            @pl.when(jnp.logical_not(relayed(s, w)))
+        return (wide[:k] + wide[k:]).astype(jnp.bfloat16)
+
+    part = width // PIECES
+
+    def hand(h, side):
+        return pltpu.make_async_remote_copy(
+            src_ref=made.at[h], dst_ref=got.at[side, h], send_sem=hs.at[side, h], recv_sem=hr.at[side, h],
+            device_id=row_id(r + 1 - 2 * side), device_id_type=MESH)
+
+    def beside(act):
+        for side in (0, 1):
+            @pl.when(r < rows - 1 if side == 0 else r > 0)
             def _():
-                unit(s, w, r).wait_recv()
-
-        def keep(g, value):
-            sbuf[w, :, lanes(g)] = value
-
-        standardize(w, keep)
-    for w in turn:
-        deliver(w, w).wait_recv()
-    for w in turn:
-        finish(w, sbuf[w])
+                act(side)
+
+    for h in range(PIECES):
+        some = slice(h * part, (h + 1) * part)
+        value = loadings(r, lhs[k:, some])
+        made[h] = value
+        beside(lambda side: hand(h, side).start())
+        out_ref[r, :, some] = value.astype(jnp.float32)
+
+    lists = [wanted(windows, x) for x in range(rows)]
+    most = max(len(v) for v in lists)
+    for act in ("scale", "expand"):
+        for j in range(most):
+            have = [x for x in range(rows) if len(lists[x]) > j]
+            w = sum(jnp.where(r == x, lists[x][j], 0) for x in have)
+
+            @pl.when(functools.reduce(jnp.logical_or, [r == x for x in have]))
+            def _():
+                if act == "expand":
+                    deliver(w, w).wait_recv()
+                    out_ref[w] = loadings(w, sbuf[j]).astype(jnp.float32)
+                    return
+
+                for d in range(1, rows):
+                    unit(row_peer(d), w, r).wait_recv()
+
+                def keep(g, value):
+                    sbuf[j, :, lanes(g)] = value
+
+                standardize(w, keep)
+
+    def collect(side):
+        for h in range(PIECES):
+            hand(h, side).wait_recv()
+            out_ref[r - 1 + 2 * side, :, h * part:(h + 1) * part] = got[side, h].astype(jnp.float32)
+
+    for side in (0, 1):
+        @pl.when(r > 0 if side == 0 else r < rows - 1)
+        def _():
+            collect(side)
+
     for c in sends:
         c.wait_send()
     for d in range(1, rows):
         gain(r, row_peer(d)).wait_send()
-    for q in order[:-1]:
-        deliver(r, q).wait_send()
-    for count in sorted({len(plan) for plan in plans}):
-        high, wide = block(count, rows, windows)
-        some = [x for x, plan in enumerate(plans) if len(plan) == count]
-
-        @pl.when(functools.reduce(jnp.logical_or, [r == x for x in some]))
-        def _():
-            whole = codes.at[pl.ds(0, high), pl.ds(0, wide)]
+
+    def settle(x):
+        for q in range(rows):
+            if abs(q - x) > 1:
+                deliver(x, q).wait_send()
+        if plans[x]:
+            whole = codes.at[pl.ds(0, len(plans[x]))]
             pltpu.make_async_remote_copy(
                 src_ref=whole, dst_ref=whole, send_sem=rest.at[0], recv_sem=cr.at[0, 0],
                 device_id=row_id(row_peer(1)), device_id_type=MESH).wait_send()
+
+    per_row(settle)
+    for h in range(PIECES):
+        beside(lambda side: hand(h, side).wait_send())
 
 
 def fused(returns, starts, start_block, rows, cols, subs):
@@ -334,17 +354,19 @@
             pltpu.VMEM(returns.shape, f32),
             pltpu.VMEM((windows, 1, width), jnp.int32),
             pltpu.VMEM((k, width), f32),
-            pltpu.VMEM((rows, windows, groups + 1, days, LANES), jnp.int16),
+            pltpu.VMEM((rows * windows, groups + 1, days, LANES), jnp.int16),
             pltpu.VMEM((k + total, width), bf16),
-            pltpu.VMEM((windows, total, width), bf16),
+            pltpu.VMEM((windows - 2, total, width), bf16),
             pltpu.VMEM((half, 2 * total), f32),
             pltpu.VMEM((mates, half, 2 * total), f32),
             pltpu.VMEM((windows, 2 * k, total), bf16),
             pltpu.VMEM((rows, windows, 1, LANES), f32),
+            pltpu.VMEM((PIECES, k, width // PIECES), bf16),
+            pltpu.VMEM((2, PIECES, k, width // PIECES), bf16),
             dma((windows,)), dma((windows + 1,)),
             dma((windows,)), dma((rows, windows)),
             dma((mates,)), dma((mates,)),
-            dma((rows,)), dma((rows,)), dma((rows,)), dma((rows,)), dma((1,)), pltpu.SemaphoreType.REGULAR,
+            dma((rows,)), dma((rows,)), dma((rows,)), dma((rows,)), dma((1,)), dma((2, PIECES)), dma((2, PIECES)), pltpu.SemaphoreType.REGULAR,
         ],
         compiler_params=pltpu.CompilerParams(collective_id=0, has_side_effects=True),
     )(returns, starts, start_block)
@@ -395,8 +417,7 @@
     windows, days, width = returns.shape
     k = start_block.shape[1]
     fits = (windows == rows and width == LANES * days and days % 16 == 0 and k % 16 == 0
-            and days * rows <= 64 and (days * rows + k) % 16 == 0 and rows > 3 and cols * subs > 1
-            and all(block(len(background(rows, windows, x)), rows, windows) for x in range(rows)))
+            and days * rows <= 64 and (days * rows + k) % 16 == 0 and rows == 4 and cols * subs > 1)
     if fits:
         return fused(returns, starts, start_block, rows, cols, subs)
     return stepwise(returns, starts, start_block, rows, cols * subs)

time: 27.6 us -> 26.3 us (0.953)
  Pallas kernels: 26.5 us -> 25.2 us
    pallas_call x1, Pallas kernels: 26.5 us -> 25.2 us  [fused(): pl.pallas_call(functools.partial(kernel, rows, cols, subs, width * mates)...]
where the time goes in v4:
time: 26.3 us; the launch traced here: 26.1 us
  Pallas kernels  25.2 us (96%)
  local copies, waits for them, and re-layouts  0.97 us (4%)
    pallas_call x1, Pallas kernels, fused(): pl.pallas_call(functools.partial(kernel, rows, cols, subs, width * mates)...  25.2 us
    unnamed x1, local copies, waits for them, and re-layouts  0.97 us

profile of v4, /device:TPU:0, one launch (start us, length us, event | category | flops | bytes accessed | tf_op | source)
XLA Modules:
  0.0 26.1 jit_solution(412240729018458636)
XLA Ops:
  0.0 25.2 %shard_map.37 = f32[4,32,2048]{2,1,0:T(8,128)S(1)} custom-call(f32[4,16,2048]{2,1,0:T(8,128)} %returns_ref.1, s32[4,2048]{1,0:T(4,128)} %starts_ref.1, f32[4,32,2048]{2,1,0:T(8,128)} %start_ref.1), custom_call_target="tpu_custom_call" | custom-call | tf_op jit(solution)/shard_map/pallas_call | solution.py:348
  25.2 1.0 %copy.5 = f32[4,32,2048]{2,1,0:T(8,128)} copy(f32[4,32,2048]{2,1,0:T(8,128)S(1)} %shard_map.37) | data formatting | bytes 2097152

commit v5 on v4

--- a/solution.py
+++ b/solution.py
@@ -54,7 +54,7 @@
 
 
 def wanted(windows, x):
-    some = [w for w in range(windows) if abs(w - x) > 1]
+    some = [w for w in range(windows) if w != x and (abs(w - x) > 1 or w in (0, windows - 1))]
     return some if x >= windows // 2 else some[::-1]
 
 
@@ -62,11 +62,19 @@
     ends = (0, rows - 1)
     plan = []
     for q in range(rows):
-        for d, w in enumerate(wanted(windows, q) if q != x else []):
-            if abs(q - x) == 1:
-                plan.append((w, q, 0 if q in ends or x in ends else 2))
-            else:
-                plan.append((w, q, 1 if q in ends and d == 0 else 2))
+        for w in wanted(windows, q) if q != x else []:
+            if q in ends:
+                plan.append((x, w, q, 0 if abs(q - x) == 1 else 1))
+            elif x in ends and abs(q - x) == 1:
+                plan.append((x, w, q, 2 if w == x else 0))
+            elif abs(q - x) == 1 and abs(w - q) > 1:
+                plan.append((x, w, q, 1))
+    if x in ends:
+        near = 1 if x == 0 else rows - 2
+        for s in range(rows):
+            if s not in (x, near):
+                plan.append((s, x, near, 2))
+                plan += [(s, w, near, 3) for w in wanted(windows, near) if w == s]
     return plan
 
 
@@ -160,9 +168,11 @@
 
     def stage(number):
         def act(x):
-            for w, q, when in plans[x]:
+            for s, w, q, when in plans[x]:
                 if when == number:
-                    unit(x, w, q, rest).start()
+                    if s != x and w != x:
+                        unit(s, w, q).wait_recv()
+                    unit(s, w, q, rest).start()
 
         per_row(act)
 
@@ -255,10 +265,11 @@
 
     def spread(x):
         for q in range(rows):
-            if abs(q - x) > 1:
+            if x in wanted(windows, q):
                 deliver(x, q).start()
 
     per_row(spread)
+    stage(3)
 
     def loadings(w, scaled):
         wide = jnp.dot(mix[w], scaled, preferred_element_type=jnp.float32)
@@ -271,17 +282,19 @@
             src_ref=made.at[h], dst_ref=got.at[side, h], send_sem=hs.at[side, h], recv_sem=hr.at[side, h],
             device_id=row_id(r + 1 - 2 * side), device_id_type=MESH)
 
-    def beside(act):
-        for side in (0, 1):
-            @pl.when(r < rows - 1 if side == 0 else r > 0)
-            def _():
-                act(side)
+    def inner(row):
+        return jnp.logical_and(row > 0, row < rows - 1)
 
     for h in range(PIECES):
         some = slice(h * part, (h + 1) * part)
         value = loadings(r, lhs[k:, some])
         made[h] = value
-        beside(lambda side: hand(h, side).start())
+
+        @pl.when(inner(r))
+        def _():
+            for side in (0, 1):
+                hand(h, side).start()
+
         out_ref[r, :, some] = value.astype(jnp.float32)
 
     lists = [wanted(windows, x) for x in range(rows)]
@@ -299,7 +312,13 @@
                     return
 
                 for d in range(1, rows):
-                    unit(row_peer(d), w, r).wait_recv()
+                    s = row_peer(d)
+
+                    @pl.when(jnp.logical_not(functools.reduce(jnp.logical_or, [
+                        jnp.logical_and(r == x, jnp.logical_and(s == p[0], w == p[1]))
+                        for x in range(rows) for p in plans[x] if p[0] != x and p[1] != x])))
+                    def _():
+                        unit(s, w, r).wait_recv()
 
                 def keep(g, value):
                     sbuf[j, :, lanes(g)] = value
@@ -312,7 +331,7 @@
             out_ref[r - 1 + 2 * side, :, h * part:(h + 1) * part] = got[side, h].astype(jnp.float32)
 
     for side in (0, 1):
-        @pl.when(r > 0 if side == 0 else r < rows - 1)
+        @pl.when(inner(r - 1 + 2 * side))
         def _():
             collect(side)
 
@@ -323,7 +342,7 @@
 
     def settle(x):
         for q in range(rows):
-            if abs(q - x) > 1:
+            if x in wanted(windows, q):
                 deliver(x, q).wait_send()
         if plans[x]:
             whole = codes.at[pl.ds(0, len(plans[x]))]
@@ -332,8 +351,11 @@
                 device_id=row_id(row_peer(1)), device_id_type=MESH).wait_send()
 
     per_row(settle)
-    for h in range(PIECES):
-        beside(lambda side: hand(h, side).wait_send())
+    @pl.when(inner(r))
+    def _():
+        for h in range(PIECES):
+            for side in (0, 1):
+                hand(h, side).wait_send()
 
 
 def fused(returns, starts, start_block, rows, cols, subs):

time: 26.3 us -> 25.8 us (0.981)
  Pallas kernels: 25.2 us -> 24.7 us
    pallas_call x1, Pallas kernels: 25.2 us -> 24.7 us  [fused(): pl.pallas_call(functools.partial(kernel, rows, cols, subs, width * mates)...]
where the time goes in v5:
time: 25.8 us; the launch traced here: 25.6 us
  Pallas kernels  24.7 us (96%)
  local copies, waits for them, and re-layouts  0.97 us (4%)
    pallas_call x1, Pallas kernels, fused(): pl.pallas_call(functools.partial(kernel, rows, cols, subs, width * mates)...  24.7 us
    unnamed x1, local copies, waits for them, and re-layouts  0.97 us

profile of v5, /device:TPU:0, one launch (start us, length us, event | category | flops | bytes accessed | tf_op | source)
XLA Modules:
  0.0 25.6 jit_solution(10644940762373229145)
XLA Ops:
  0.0 24.7 %shard_map.37 = f32[4,32,2048]{2,1,0:T(8,128)S(1)} custom-call(f32[4,16,2048]{2,1,0:T(8,128)} %returns_ref.1, s32[4,2048]{1,0:T(4,128)} %starts_ref.1, f32[4,32,2048]{2,1,0:T(8,128)} %start_ref.1), custom_call_target="tpu_custom_call" | custom-call | tf_op jit(solution)/shard_map/pallas_call | solution.py:370
  24.7 1.0 %copy.5 = f32[4,32,2048]{2,1,0:T(8,128)} copy(f32[4,32,2048]{2,1,0:T(8,128)S(1)} %shard_map.37) | data formatting | bytes 2097152

commit v6 on v5

--- a/solution.py
+++ b/solution.py
@@ -81,7 +81,7 @@
 def kernel(rows, cols, subs, assets,
            returns_ref, starts_ref, start_ref, out_ref,
            held, begins, firsts, codes, lhs, sbuf, mine, quad, mix, gains, made, got,
-           ls, bs, cs, cr, qs, qr, ms, mr, gs, gr, rest, hs, hr, clear):
+           ls, bs, cs, pr, cr, rr, qs, qr, ms, mr, gs, gr, rest, hs, hr, clear):
     r = lax.axis_index("rows")
     mates = cols * subs
     m = lax.axis_index("cols") * subs + lax.axis_index("sub")
@@ -106,13 +106,13 @@
         return slice(g * LANES, (g + 1) * LANES)
 
     order = [row_peer(d) for d in sorted(range(rows), key=lambda d: -min(d, rows - d))]
-    load_begins = [pltpu.make_async_copy(starts_ref.at[pl.ds(w, 1)], begins.at[w], bs.at[w]) for w in range(windows)]
+    load_begins = [pltpu.make_async_copy(starts_ref.at[pl.ds(w, 1)], begins.at[w], bs.at[0]) for w in range(windows)]
     for c in load_begins:
         c.start()
     loads = [pltpu.make_async_copy(returns_ref.at[w], held.at[w], ls.at[w]) for w in order]
     for c in loads:
         c.start()
-    load_firsts = pltpu.make_async_copy(start_ref.at[r], firsts, bs.at[windows])
+    load_firsts = pltpu.make_async_copy(start_ref.at[r], firsts, bs.at[1])
     load_firsts.start()
 
     barrier = pltpu.get_barrier_semaphore()
@@ -121,16 +121,35 @@
     for d in range(1, mates):
         pl.semaphore_signal(barrier, inc=1, device_id=mate_id(mate(d)), device_id_type=MESH)
 
-    def unit(s, w, q, sem=None):
+    cuts = (0, 1 + groups // 2, 1 + groups)
+
+    def received(sem, *region):
+        whole = codes.at[region]
+        pltpu.make_async_remote_copy(
+            src_ref=whole, dst_ref=whole, send_sem=cs.at[0], recv_sem=sem,
+            device_id=row_id(row_peer(1)), device_id_type=MESH).wait_recv()
+
+    def sent(sem, ref):
+        pltpu.make_async_remote_copy(
+            src_ref=ref, dst_ref=ref, send_sem=sem, recv_sem=rr.at[0],
+            device_id=row_id(row_peer(1)), device_id_type=MESH).wait_send()
+
+    def half_unit(w, h):
+        tiles = codes.at[r * windows + w, pl.ds(cuts[h], cuts[h + 1] - cuts[h])]
+        return pltpu.make_async_remote_copy(
+            src_ref=tiles, dst_ref=tiles, send_sem=cs.at[0], recv_sem=pr.at[h],
+            device_id=row_id(w), device_id_type=MESH)
+
+    def unit(s, w, q, relay):
         return pltpu.make_async_remote_copy(
             src_ref=codes.at[s * windows + w], dst_ref=codes.at[s * windows + w],
-            send_sem=cs.at[w] if sem is None else sem.at[0], recv_sem=cr.at[s, w],
+            send_sem=rest.at[0], recv_sem=rr.at[0] if relay else cr.at[w],
             device_id=row_id(q), device_id_type=MESH)
 
     def gain(s, q):
         return pltpu.make_async_remote_copy(
-            src_ref=gains.at[s], dst_ref=gains.at[s], send_sem=gs.at[q],
-            recv_sem=gr.at[s], device_id=row_id(q), device_id_type=MESH)
+            src_ref=gains.at[s], dst_ref=gains.at[s], send_sem=gs.at[0],
+            recv_sem=gr.at[0], device_id=row_id(q), device_id_type=MESH)
 
     row = lax.broadcasted_iota(jnp.int32, (groups, LANES), 0)
     own_day = r * days + lax.broadcasted_iota(jnp.int32, (days, LANES), 0)
@@ -152,11 +171,11 @@
             reach = jnp.maximum(reach, jnp.maximum(top - middle, middle - low))
             centers = jnp.where(row == g, center, centers)
             middles.append(middle)
-        codes[r * windows + w, groups] = centers.astype(jnp.int32).astype(jnp.int16)
+        codes[r * windows + w, 0] = centers.astype(jnp.int32).astype(jnp.int16)
         gains[r, w] = reach * (1.0 / TOP)
         inverse = TOP / reach
         for g in range(groups):
-            codes[r * windows + w, g] = jnp.round((load(g) - middles[g]) * inverse).astype(jnp.int32).astype(jnp.int16)
+            codes[r * windows + w, 1 + g] = jnp.round((load(g) - middles[g]) * inverse).astype(jnp.int32).astype(jnp.int16)
 
     plans = [background(rows, windows, x) for x in range(rows)]
 
@@ -171,28 +190,28 @@
             for s, w, q, when in plans[x]:
                 if when == number:
                     if s != x and w != x:
-                        unit(s, w, q).wait_recv()
-                    unit(s, w, q, rest).start()
+                        received(rr.at[0], s * windows + w)
+                    unit(s, w, q, s == x == w and abs(q - x) == rows - 1).start()
 
         per_row(act)
 
-    for c in load_begins:
-        c.wait()
+    pltpu.make_async_copy(begins, begins, bs.at[0]).wait()
     for i, w in enumerate(order):
         loads[i].wait()
         encode(w)
         if i == 1:
             pl.semaphore_wait(barrier, rows - 1 + mates - 1)
         if i > 0:
-            unit(r, order[i - 1], order[i - 1]).start()
+            half_unit(order[i - 1], 0).start()
+    for w in order[:-1]:
+        half_unit(w, 1).start()
     for d in range(1, rows):
         gain(r, row_peer(d)).start()
     stage(0)
 
     load_firsts.wait()
     lhs[:k] = firsts[...].astype(jnp.bfloat16)
-    for w in order[:-1]:
-        unit(r, w, w).wait_send()
+    sent(cs.at[0], codes.at[pl.ds(0, rows - 1)])
     for d in range(1, subs):
         pl.semaphore_signal(clear, inc=1, device_id={"sub": lax.rem(lax.axis_index("sub") + d, subs)},
                             device_id_type=MESH)
@@ -201,12 +220,12 @@
 
     day = lax.broadcasted_iota(jnp.int32, (total, LANES), 0)
 
-    def standardize(w, store):
-        middles = [codes[s * windows + w, groups].astype(jnp.float32) * (LIMIT / TOP) for s in range(rows)]
+    def standardize(w, store, some=range(groups)):
+        middles = [codes[s * windows + w, 0].astype(jnp.float32) * (LIMIT / TOP) for s in range(rows)]
         steps = [gains[s, w] for s in range(rows)]
-        for g in range(groups):
+        for g in some:
             x = jnp.concatenate([
-                codes[s * windows + w, g].astype(jnp.float32) * steps[s] + middles[s][g:g + 1]
+                codes[s * windows + w, 1 + g].astype(jnp.float32) * steps[s] + middles[s][g:g + 1]
                 for s in range(rows)], axis=0)
             begin = begins[w, :, lanes(g)]
             live = day >= begin
@@ -216,31 +235,31 @@
             squares = jnp.sum(centered * centered, axis=0, keepdims=True)
             store(g, (centered * lax.rsqrt(squares + 1.0)).astype(jnp.bfloat16))
 
-    for d in range(1, rows):
-        gain(row_peer(d), r).wait_recv()
-        unit(row_peer(d), r, r).wait_recv()
     def keep_own(g, value):
         lhs[k:, lanes(g)] = value
 
-    standardize(r, keep_own)
-    sums = lax.dot_general(lhs[...], lhs[k:], NT, preferred_element_type=jnp.float32)
+    some_gains = gains.at[pl.ds(0, rows - 1)]
+    pltpu.make_async_remote_copy(
+        src_ref=some_gains, dst_ref=some_gains, send_sem=gs.at[0], recv_sem=gr.at[0],
+        device_id=row_id(row_peer(1)), device_id_type=MESH).wait_recv()
+    sums = jnp.zeros((k + total, total), jnp.float32)
+    for h in range(2):
+        received(pr.at[h], pl.ds(0, rows - 1), pl.ds(cuts[h], cuts[h + 1] - cuts[h]))
+        standardize(r, keep_own, range(h * groups // 2, (h + 1) * groups // 2))
+        side = slice(h * width // 2, (h + 1) * width // 2)
+        sums = sums + lax.dot_general(lhs[:, side], lhs[k:, side], NT, preferred_element_type=jnp.float32)
     summed = jnp.concatenate([sums[:half], sums[half:]], axis=1)
     mine[...] = summed
-    sends = []
     for d in range(1, mates):
-        q = mate(d)
-        c = pltpu.make_async_remote_copy(
-            src_ref=mine, dst_ref=quad.at[m], send_sem=qs.at[d], recv_sem=qr.at[m],
-            device_id=mate_id(q), device_id_type=MESH)
-        c.start()
-        sends.append(c)
+        pltpu.make_async_remote_copy(
+            src_ref=mine, dst_ref=quad.at[m], send_sem=qs.at[0], recv_sem=qr.at[0],
+            device_id=mate_id(mate(d)), device_id_type=MESH).start()
     quad[m] = summed
     stage(2)
-    for d in range(1, mates):
-        q = mate(d)
-        pltpu.make_async_remote_copy(
-            src_ref=mine, dst_ref=quad.at[q], send_sem=qs.at[d], recv_sem=qr.at[q],
-            device_id=mate_id(q), device_id_type=MESH).wait_recv()
+    others = pltpu.make_async_remote_copy(
+        src_ref=quad.at[pl.ds(0, mates - 1)], dst_ref=quad.at[pl.ds(0, mates - 1)],
+        send_sem=qs.at[0], recv_sem=qr.at[0], device_id=mate_id(mate(1)), device_id_type=MESH)
+    others.wait_recv()
     both = quad[0]
     for q in range(1, mates):
         both = both + quad[q]
@@ -260,7 +279,7 @@
 
     def deliver(slot, q):
         return pltpu.make_async_remote_copy(
-            src_ref=mix.at[slot], dst_ref=mix.at[slot], send_sem=ms.at[q], recv_sem=mr.at[slot],
+            src_ref=mix.at[slot], dst_ref=mix.at[slot], send_sem=ms.at[0], recv_sem=mr.at[slot],
             device_id=row_id(q), device_id_type=MESH)
 
     def spread(x):
@@ -279,7 +298,7 @@
 
     def hand(h, side):
         return pltpu.make_async_remote_copy(
-            src_ref=made.at[h], dst_ref=got.at[side, h], send_sem=hs.at[side, h], recv_sem=hr.at[side, h],
+            src_ref=made.at[h], dst_ref=got.at[side, h], send_sem=hs.at[0], recv_sem=hr.at[side, h],
             device_id=row_id(r + 1 - 2 * side), device_id_type=MESH)
 
     def inner(row):
@@ -311,14 +330,12 @@
                     out_ref[w] = loadings(w, sbuf[j]).astype(jnp.float32)
                     return
 
-                for d in range(1, rows):
-                    s = row_peer(d)
-
-                    @pl.when(jnp.logical_not(functools.reduce(jnp.logical_or, [
-                        jnp.logical_and(r == x, jnp.logical_and(s == p[0], w == p[1]))
-                        for x in range(rows) for p in plans[x] if p[0] != x and p[1] != x])))
+                part_only = [x for x in have if any(p[0] != x and p[1] == lists[x][j] for p in plans[x] if p[3] == 3)]
+                fewer = functools.reduce(jnp.logical_or, [r == x for x in part_only], False)
+                for count, flag in ((rows - 2, fewer), (rows - 1, jnp.logical_not(fewer))):
+                    @pl.when(flag)
                     def _():
-                        unit(s, w, r).wait_recv()
+                        received(cr.at[w], pl.ds(0, count))
 
                 def keep(g, value):
                     sbuf[j, :, lanes(g)] = value
@@ -335,27 +352,19 @@
         def _():
             collect(side)
 
-    for c in sends:
-        c.wait_send()
-    for d in range(1, rows):
-        gain(r, row_peer(d)).wait_send()
+    others.wait_send()
+    sent(gs.at[0], gains.at[pl.ds(0, rows - 1)])
 
     def settle(x):
-        for q in range(rows):
-            if x in wanted(windows, q):
-                deliver(x, q).wait_send()
-        if plans[x]:
-            whole = codes.at[pl.ds(0, len(plans[x]))]
-            pltpu.make_async_remote_copy(
-                src_ref=whole, dst_ref=whole, send_sem=rest.at[0], recv_sem=cr.at[0, 0],
-                device_id=row_id(row_peer(1)), device_id_type=MESH).wait_send()
+        count = sum(x in wanted(windows, q) for q in range(rows))
+        sent(ms.at[0], mix.at[pl.ds(0, count)])
+        sent(rest.at[0], codes.at[pl.ds(0, len(plans[x]))])
 
     per_row(settle)
+
     @pl.when(inner(r))
     def _():
-        for h in range(PIECES):
-            for side in (0, 1):
-                hand(h, side).wait_send()
+        sent(hs.at[0], got)
 
 
 def fused(returns, starts, start_block, rows, cols, subs):
@@ -385,10 +394,11 @@
             pltpu.VMEM((rows, windows, 1, LANES), f32),
             pltpu.VMEM((PIECES, k, width // PIECES), bf16),
             pltpu.VMEM((2, PIECES, k, width // PIECES), bf16),
-            dma((windows,)), dma((windows + 1,)),
-            dma((windows,)), dma((rows, windows)),
-            dma((mates,)), dma((mates,)),
-            dma((rows,)), dma((rows,)), dma((rows,)), dma((rows,)), dma((1,)), dma((2, PIECES)), dma((2, PIECES)), pltpu.SemaphoreType.REGULAR,
+            dma((windows,)), dma((2,)),
+            dma((1,)), dma((2,)), dma((windows,)), dma((1,)),
+            dma((1,)), dma((1,)), dma((1,)), dma((windows,)),
+            dma((1,)), dma((1,)), dma((1,)), dma((1,)), dma((2, PIECES)),
+            pltpu.SemaphoreType.REGULAR,
         ],
         compiler_params=pltpu.CompilerParams(collective_id=0, has_side_effects=True),
     )(returns, starts, start_block)

time: 25.8 us -> 25.6 us (level)
  no operation moved by 1% of the time
where the time goes in v6:
time: 25.6 us; the launch traced here: 25.4 us
  Pallas kernels  24.5 us (96%)
  local copies, waits for them, and re-layouts  0.97 us (4%)
    pallas_call x1, Pallas kernels, fused(): pl.pallas_call(functools.partial(kernel, rows, cols, subs, width * mates)...  24.5 us
    unnamed x1, local copies, waits for them, and re-layouts  0.97 us

profile of v6, /device:TPU:0, one launch (start us, length us, event | category | flops | bytes accessed | tf_op | source)
XLA Modules:
  0.0 25.4 jit_solution(8639454921709890146)
XLA Ops:
  0.0 24.5 %shard_map.37 = f32[4,32,2048]{2,1,0:T(8,128)S(1)} custom-call(f32[4,16,2048]{2,1,0:T(8,128)} %returns_ref.1, s32[4,2048]{1,0:T(4,128)} %starts_ref.1, f32[4,32,2048]{2,1,0:T(8,128)} %start_ref.1), custom_call_target="tpu_custom_call" | custom-call | tf_op jit(solution)/shard_map/pallas_call | solution.py:379
  24.5 1.0 %copy.5 = f32[4,32,2048]{2,1,0:T(8,128)} copy(f32[4,32,2048]{2,1,0:T(8,128)S(1)} %shard_map.37) | data formatting | bytes 2097152

commit v7 on v6

--- a/solution.py
+++ b/solution.py
@@ -81,7 +81,7 @@
 def kernel(rows, cols, subs, assets,
            returns_ref, starts_ref, start_ref, out_ref,
            held, begins, firsts, codes, lhs, sbuf, mine, quad, mix, gains, made, got,
-           ls, bs, cs, pr, cr, rr, qs, qr, ms, mr, gs, gr, rest, hs, hr, clear):
+           ls, bs, cs, pr, cr, rr, qs, qr, ms, mr, gs, gr, rest, hs, hr, clear, ready):
     r = lax.axis_index("rows")
     mates = cols * subs
     m = lax.axis_index("cols") * subs + lax.axis_index("sub")
@@ -116,8 +116,11 @@
     load_firsts.start()
 
     barrier = pltpu.get_barrier_semaphore()
-    for d in range(1, rows):
-        pl.semaphore_signal(barrier, inc=1, device_id=row_id(row_peer(d)), device_id_type=MESH)
+    for step in (1, -1):
+        @pl.when(r + step < rows if step > 0 else r > 0)
+        def _():
+            pl.semaphore_signal(barrier, inc=1, device_id=row_id(r + step), device_id_type=MESH)
+
     for d in range(1, mates):
         pl.semaphore_signal(barrier, inc=1, device_id=mate_id(mate(d)), device_id_type=MESH)
 
@@ -185,10 +188,10 @@
             def _():
                 act(x)
 
-    def stage(number):
+    def stage(number, some=range(rows)):
         def act(x):
             for s, w, q, when in plans[x]:
-                if when == number:
+                if when == number and x in some:
                     if s != x and w != x:
                         received(rr.at[0], s * windows + w)
                     unit(s, w, q, s == x == w and abs(q - x) == rows - 1).start()
@@ -199,15 +202,28 @@
     for i, w in enumerate(order):
         loads[i].wait()
         encode(w)
-        if i == 1:
-            pl.semaphore_wait(barrier, rows - 1 + mates - 1)
-        if i > 0:
-            half_unit(order[i - 1], 0).start()
-    for w in order[:-1]:
-        half_unit(w, 1).start()
-    for d in range(1, rows):
-        gain(r, row_peer(d)).start()
-    stage(0)
+    pl.semaphore_wait(barrier, mates - 1 + jnp.where(jnp.logical_or(r == 0, r == rows - 1), 1, 2))
+
+    def reach_out(x):
+        for t in range(1, rows):
+            for step in (1, -1):
+                if 0 <= x - step * t < rows and 0 <= x + step < rows and t + 1 < rows:
+                    pl.semaphore_signal(ready.at[0 if step > 0 else 1, t + 1], inc=1,
+                                        device_id=row_id(x + step), device_id_type=MESH)
+            for q in (x + t, x - t):
+                if 0 <= q < rows:
+                    half_unit(q, 0).start()
+                    half_unit(q, 1).start()
+                    gain(r, q).start()
+            if t == (rows - 1 if x in (0, rows - 1) else 1):
+                for s, w, q, when in plans[x]:
+                    if when == 0:
+                        unit(s, w, q, False).start()
+            for side, far in ((0, x - t - 1), (1, x + t + 1)):
+                if 0 <= far < rows:
+                    pl.semaphore_wait(ready.at[side, t + 1], 1)
+
+    per_row(reach_out)
 
     load_firsts.wait()
     lhs[:k] = firsts[...].astype(jnp.bfloat16)
@@ -216,7 +232,8 @@
         pl.semaphore_signal(clear, inc=1, device_id={"sub": lax.rem(lax.axis_index("sub") + d, subs)},
                             device_id_type=MESH)
     pl.semaphore_wait(clear, subs - 1)
-    stage(1)
+    held_back = (0, rows - 2)
+    stage(1, [x for x in range(rows) if x not in held_back])
 
     day = lax.broadcasted_iota(jnp.int32, (total, LANES), 0)
 
@@ -245,6 +262,8 @@
     sums = jnp.zeros((k + total, total), jnp.float32)
     for h in range(2):
         received(pr.at[h], pl.ds(0, rows - 1), pl.ds(cuts[h], cuts[h + 1] - cuts[h]))
+        if h == 1:
+            stage(1, held_back)
         standardize(r, keep_own, range(h * groups // 2, (h + 1) * groups // 2))
         side = slice(h * width // 2, (h + 1) * width // 2)
         sums = sums + lax.dot_general(lhs[:, side], lhs[k:, side], NT, preferred_element_type=jnp.float32)
@@ -398,7 +417,7 @@
             dma((1,)), dma((2,)), dma((windows,)), dma((1,)),
             dma((1,)), dma((1,)), dma((1,)), dma((windows,)),
             dma((1,)), dma((1,)), dma((1,)), dma((1,)), dma((2, PIECES)),
-            pltpu.SemaphoreType.REGULAR,
+            pltpu.SemaphoreType.REGULAR, pltpu.SemaphoreType.REGULAR((2, rows)),
         ],
         compiler_params=pltpu.CompilerParams(collective_id=0, has_side_effects=True),
     )(returns, starts, start_block)

time: 25.6 us -> 24.5 us (0.957)
  Pallas kernels: 24.5 us -> 23.4 us
    pallas_call x1, Pallas kernels: 24.5 us -> 23.4 us  [fused(): pl.pallas_call(functools.partial(kernel, rows, cols, subs, width * mates)...]
where the time goes in v7:
time: 24.5 us; the launch traced here: 24.4 us
  Pallas kernels  23.4 us (96%)
  local copies, waits for them, and re-layouts  0.97 us (4%)
    pallas_call x1, Pallas kernels, fused(): pl.pallas_call(functools.partial(kernel, rows, cols, subs, width * mates)...  23.4 us
    unnamed x1, local copies, waits for them, and re-layouts  0.97 us

profile of v7, /device:TPU:0, one launch (start us, length us, event | category | flops | bytes accessed | tf_op | source)
XLA Modules:
  0.0 24.4 jit_solution(9659055602099924667)
XLA Ops:
  0.0 23.4 %shard_map.37 = f32[4,32,2048]{2,1,0:T(8,128)S(1)} custom-call(f32[4,16,2048]{2,1,0:T(8,128)} %returns_ref.1, s32[4,2048]{1,0:T(4,128)} %starts_ref.1, f32[4,32,2048]{2,1,0:T(8,128)} %start_ref.1), custom_call_target="tpu_custom_call" | custom-call | tf_op jit(solution)/shard_map/pallas_call | solution.py:398
  23.4 1.0 %copy.5 = f32[4,32,2048]{2,1,0:T(8,128)} copy(f32[4,32,2048]{2,1,0:T(8,128)S(1)} %shard_map.37) | data formatting | bytes 2097152

commit v8 on v7

--- a/solution.py
+++ b/solution.py
@@ -232,7 +232,7 @@
         pl.semaphore_signal(clear, inc=1, device_id={"sub": lax.rem(lax.axis_index("sub") + d, subs)},
                             device_id_type=MESH)
     pl.semaphore_wait(clear, subs - 1)
-    held_back = (0, rows - 2)
+    held_back = (0,)
     stage(1, [x for x in range(rows) if x not in held_back])
 
     day = lax.broadcasted_iota(jnp.int32, (total, LANES), 0)
@@ -335,7 +335,7 @@
 
         out_ref[r, :, some] = value.astype(jnp.float32)
 
-    lists = [wanted(windows, x) for x in range(rows)]
+    lists = [wanted(windows, x)[::1 if x in (0, rows - 1) else -1] for x in range(rows)]
     most = max(len(v) for v in lists)
     for act in ("scale", "expand"):
         for j in range(most):

time: 24.5 us -> 24.3 us (level)
  no operation moved by 1% of the time
where the time goes in v8:
time: 24.3 us; the launch traced here: 24.2 us
  Pallas kernels  23.2 us (95%)
  local copies, waits for them, and re-layouts  0.97 us (4%)
    pallas_call x1, Pallas kernels, fused(): pl.pallas_call(functools.partial(kernel, rows, cols, subs, width * mates)...  23.2 us
    unnamed x1, local copies, waits for them, and re-layouts  0.97 us

profile of v8, /device:TPU:0, one launch (start us, length us, event | category | flops | bytes accessed | tf_op | source)
XLA Modules:
  0.0 24.2 jit_solution(14566459053675083437)
XLA Ops:
  0.0 23.2 %shard_map.37 = f32[4,32,2048]{2,1,0:T(8,128)S(1)} custom-call(f32[4,16,2048]{2,1,0:T(8,128)} %returns_ref.1, s32[4,2048]{1,0:T(4,128)} %starts_ref.1, f32[4,32,2048]{2,1,0:T(8,128)} %start_ref.1), custom_call_target="tpu_custom_call" | custom-call | tf_op jit(solution)/shard_map/pallas_call | solution.py:398
  23.2 1.0 %copy.5 = f32[4,32,2048]{2,1,0:T(8,128)} copy(f32[4,32,2048]{2,1,0:T(8,128)S(1)} %shard_map.37) | data formatting | bytes 2097152

commit v9 on v8

--- a/solution.py
+++ b/solution.py
@@ -215,7 +215,7 @@
                     half_unit(q, 0).start()
                     half_unit(q, 1).start()
                     gain(r, q).start()
-            if t == (rows - 1 if x in (0, rows - 1) else 1):
+            if t == (rows - 1 if x in (0, rows - 1) else 2):
                 for s, w, q, when in plans[x]:
                     if when == 0:
                         unit(s, w, q, False).start()

time: 24.3 us -> 24.3 us (level)
  no operation moved by 1% of the time
where the time goes in v9:
time: 24.3 us; the launch traced here: 24.2 us
  Pallas kernels  23.2 us (95%)
  local copies, waits for them, and re-layouts  0.97 us (4%)
    pallas_call x1, Pallas kernels, fused(): pl.pallas_call(functools.partial(kernel, rows, cols, subs, width * mates)...  23.2 us
    unnamed x1, local copies, waits for them, and re-layouts  0.97 us

profile of v9, /device:TPU:0, one launch (start us, length us, event | category | flops | bytes accessed | tf_op | source)
XLA Modules:
  0.0 24.2 jit_solution(16377554093866534721)
XLA Ops:
  0.0 23.2 %shard_map.37 = f32[4,32,2048]{2,1,0:T(8,128)S(1)} custom-call(f32[4,16,2048]{2,1,0:T(8,128)} %returns_ref.1, s32[4,2048]{1,0:T(4,128)} %starts_ref.1, f32[4,32,2048]{2,1,0:T(8,128)} %start_ref.1), custom_call_target="tpu_custom_call" | custom-call | tf_op jit(solution)/shard_map/pallas_call | solution.py:398
  23.2 1.0 %copy.5 = f32[4,32,2048]{2,1,0:T(8,128)} copy(f32[4,32,2048]{2,1,0:T(8,128)S(1)} %shard_map.37) | data formatting | bytes 2097152
